TPU v7x, 512 devices: a 4x2x32 block of a 4x8x32 slice. The times are simulated.
512 devices in a mesh: groups: 2 (over y), head: 64 (over z, core), state: 4 (over x).
Axes of the slice: x: 4, y: 2, z: 32, core: 2. Of those that a mesh axis runs over, the one named last changes fastest.
The devices are a block of a 4x8x32 slice.
Arguments:
- tokens: bfloat16 [512, 2048], P(('groups', 'head'), 'state'), parts along dimension 0, may hold values from -20 to 20
- mixer_norm: float32 [2048], P('state'), may hold values from 0.1 to 1.9
- input_proj: bfloat16 [2, 2048, 8192], P(None, 'state', 'head'), may hold values from -0.125 to 0.125
- conv_weight: float32 [4, 8192], P(None, 'head'), may hold values from -3 to 3
- conv_bias: float32 [8192], P('head'), may hold values from -3 to 3
- conv_state: float32 [3, 512, 8192], P(None, 'groups', 'head'), parts along dimension 1, may hold values from -6 to 6
- state_proj: bfloat16 [8192, 288], P('head'), may hold values from -0.125 to 0.125
- step_gain: float32 [256], replicated, may hold values from 0.1 to 1.9
- step_proj: bfloat16 [256, 8192], P(None, 'head'), may hold values from -0.375 to 0.375
- step_bias: float32 [8192], P('head'), may hold values from -6 to -1
- decay_log: float32 [16, 8192], P('state', 'head'), may hold values from 0 to 2.77
- skip_gain: float32 [8192], P('head'), may hold values from 0.5 to 1.5
- ssm_state: float32 [16, 512, 8192], P('state', 'groups', 'head'), parts along dimension 1, may hold values from -6 to 6
- output_proj: bfloat16 [8192, 2048], P('head', 'state'), may hold values from -0.0625 to 0.0625
- moe_norm: float32 [2048], replicated, may hold values from 0.1 to 1.9
- router_weight: float32 [2048, 8], replicated, may hold values from -0.125 to 0.125
- expert_ids: int32 [512, 2], P(('groups', 'head')), parts along dimension 0, may hold values from 0 to 7, as said below
- slot_ids: int32 [512, 2], P(('groups', 'head')), parts along dimension 0, may hold values from 0 to 3, as said below
- gate_proj: bfloat16 [64, 2048, 896], P('head', None, 'state'), may hold values from -0.125 to 0.125
- up_proj: bfloat16 [64, 2048, 896], P('head', None, 'state'), may hold values from -0.125 to 0.125
- down_proj: bfloat16 [64, 896, 2048], P('head', 'state'), may hold values from -0.0625 to 0.0625
Outputs:
- layer_out: bfloat16 [512, 2048], P(('groups', 'head'), 'state'), parts along dimension 0
- new_conv: float32 [3, 512, 8192], P(None, 'groups', 'head'), parts along dimension 1
- new_state: float32 [16, 512, 8192], P('state', 'groups', 'head'), parts along dimension 1
- expert_load: float32 [16], P('groups'), parts along dimension 0
- aux_loss: float32 [2], P('groups'), parts along dimension 0
There are 2 independent parts, one for each index of `groups`. A program takes and returns all parts, laid end to end along the dimension named above; an argument that names none is the same for every part. Nothing has to cross between parts.
Inputs may be any that keep to these rules, and one draw needn't show every extreme that they name: `expert_ids`: each row names 2 different experts. One expert, the same on every device, is named by every row. `slot_ids`: among the choices of one aligned block of 4 rows that name one expert, the slot positions are distinct and run from 0 to their count less one.
All inputs are finite; a program needn't handle non-finite values.
Results may differ from a plain program's by a relative error of at most 0.007.
Values may be sent and summed in bfloat16 or wider, within the bound.
A program may use at most 64 MiB of HBM per device.

v0:
```python
import functools

import jax
import jax.numpy as jnp
from jax import lax
from jax.sharding import Mesh
from jax.sharding import PartitionSpec as P

D = 2048
D_STATE = 16
DT_RANK = 256
EXPERTS = 8
TOPK = 2
CAP = 2
HEAD = ("head_0", "head_1")
GROUPS_HEAD = ("groups", "head_0", "head_1")


NORM_EPS = 1e-05
STEP_EPS = 1e-06


def copy_for_each(shard, axis):
    length = lax.axis_size(axis)
    return lax.all_to_all(
        jnp.broadcast_to(shard[None], (length, *shard.shape)), axis, 0, 0, tiled=True
    )


def over_copies(shard, axis):
    return copy_for_each(shard, axis).sum(axis=0)


def laid_out(tiles, dim):
    tiles = jnp.moveaxis(tiles, 0, dim)
    shape = tiles.shape
    return tiles.reshape(*shape[:dim], shape[dim] * shape[dim + 1], *shape[dim + 2 :])


def gather_in_order(shard, axes, sequence):
    tiles = shard
    for k in sequence:
        tiles = lax.all_gather(tiles, axes[k])
    done = sequence[::-1]
    back = [done.index(k) for k in range(len(axes))]
    tiles = tiles.transpose(*back, *range(len(axes), tiles.ndim))
    return tiles.reshape(-1, *shard.shape)


def gathered_by_axis(shard, axes, sequence, dim):
    return laid_out(gather_in_order(shard, axes, sequence), dim)


def over_axes_2(shard, axes):
    return functools.reduce(lax.psum, axes, shard)


def in_blocks(shard, dim, length):
    shape = shard.shape
    tiles = shard.reshape(*shape[:dim], length, shape[dim] // length, *shape[dim + 1 :])
    return jnp.moveaxis(tiles, dim, 0)


def sent_and_summed(shard, axis, dim):
    tiles = in_blocks(shard, dim, lax.axis_size(axis))
    arrived = lax.all_to_all(tiles, axis, split_axis=0, concat_axis=0, tiled=True)
    return arrived.sum(axis=0)


def in_one(arrays, axis):
    ravelled, at, outs = (jnp.concatenate([a.reshape(-1) for a in arrays]), 0, [])
    running = over_copies(ravelled, axis)
    for a in arrays:
        outs.append(running[at : at + a.size].reshape(a.shape))
        at += a.size
    return tuple(outs)


def collect(shard, axis, dim):
    return laid_out(copy_for_each(shard, axis), dim)


def sum_at_owner(shard, axis, dim):
    tiles = in_blocks(shard, dim, lax.axis_size(axis))
    arrived = lax.all_to_all(tiles, axis, split_axis=0, concat_axis=0, tiled=True)
    return arrived.astype(jnp.float32).sum(axis=0)


def expert_ffn(received, gate_proj, up_proj, down_proj):
    gate_val = jnp.einsum("nlcd,ldf->nlcf", received, gate_proj, preferred_element_type=jnp.float32)
    up_val = jnp.einsum("nlcd,ldf->nlcf", received, up_proj, preferred_element_type=jnp.float32)
    hidden = (jax.nn.silu(gate_val) * up_val).astype(jnp.bfloat16)
    return jnp.einsum("nlcf,lfd->nlcd", hidden, down_proj, preferred_element_type=jnp.float32)


def per_device(
    tokens,
    mixer_norm,
    input_proj,
    conv_weight,
    conv_bias,
    conv_state,
    state_proj,
    step_gain,
    step_proj,
    step_bias,
    decay_log,
    skip_gain,
    ssm_state,
    output_proj,
    moe_norm,
    router_weight,
    expert_ids,
    slot_ids,
    gate_proj,
    up_proj,
    down_proj,
):
    head_count = lax.axis_size(HEAD)
    state_index = lax.axis_index("state")
    own_rows = tokens.shape[0]
    quarter = tokens.shape[1]
    tok_f32 = tokens.astype(jnp.float32)
    first_sq = over_copies(jnp.sum(tok_f32 * tok_f32, axis=1), "state")
    inv_first = lax.rsqrt(first_sq / D + NORM_EPS)[:, None]
    normed = (tok_f32 * inv_first * mixer_norm).astype(jnp.bfloat16)
    branch_part = jnp.einsum(
        "td,kdc->ktc",
        gathered_by_axis(normed, HEAD, (0, 1), 0),
        input_proj,
        preferred_element_type=jnp.float32,
    )
    branch_full = over_copies(branch_part, "state")
    conv_input = branch_full[0]
    gate_branch = branch_full[1]
    window = jnp.concatenate([conv_state, conv_input[None]], axis=0)
    conv_out = jax.nn.silu(jnp.sum(conv_weight[:, None, :] * window, axis=0) + conv_bias)
    new_conv = window[1:]
    proj_part = jnp.dot(
        conv_out.astype(jnp.bfloat16), state_proj, preferred_element_type=jnp.float32
    )
    projected = over_axes_2(proj_part, HEAD)
    step_low = projected[:, :DT_RANK]
    state_slab = decay_log.shape[0]
    b_input = lax.dynamic_slice_in_dim(projected, DT_RANK + state_index * state_slab, state_slab, 1)
    c_output = lax.dynamic_slice_in_dim(
        projected, DT_RANK + D_STATE + state_index * state_slab, state_slab, 1
    )
    step_inv = lax.rsqrt(jnp.mean(step_low * step_low, axis=1, keepdims=True) + STEP_EPS)
    step_normed = (step_low * step_inv * step_gain).astype(jnp.bfloat16)
    step_size = jax.nn.softplus(
        jnp.dot(step_normed, step_proj, preferred_element_type=jnp.float32) + step_bias
    )
    decay_rate = jnp.exp(-step_size[None] * jnp.exp(decay_log)[:, None, :])
    new_state = decay_rate * ssm_state + step_size[None] * b_input.T[:, :, None] * conv_out[None]
    read_part = jnp.sum(c_output.T[:, :, None] * new_state, axis=0)
    readout = over_copies(read_part, "state")
    mixer_act = ((readout + skip_gain * conv_out) * jax.nn.silu(gate_branch)).astype(jnp.bfloat16)
    mixer_sum = sent_and_summed(
        jnp.dot(mixer_act, output_proj, preferred_element_type=jnp.float32), HEAD, 0
    )
    residual = (tok_f32 + mixer_sum).astype(jnp.bfloat16)
    resid_f32 = residual.astype(jnp.float32)
    gain_part = lax.dynamic_slice_in_dim(moe_norm, state_index * quarter, quarter, 0)
    router_part = lax.dynamic_slice_in_dim(router_weight, state_index * quarter, quarter, 0)
    scaled = resid_f32 * gain_part
    own_sq = jnp.sum(resid_f32 * resid_f32, axis=1)
    raw_part = jnp.dot(scaled, router_part, precision=lax.Precision.HIGHEST)
    second_sq, raw_logits = in_one((own_sq, raw_part), "state")
    inv_second = lax.rsqrt(second_sq / D + NORM_EPS)[:, None]
    logits = inv_second * raw_logits
    row_normed = (scaled * inv_second).astype(jnp.bfloat16)
    expert_hit = expert_ids[:, :, None] == jnp.arange(EXPERTS, dtype=jnp.int32)[None, None, :]
    chosen = jnp.sum(jnp.where(expert_hit, logits[:, None, :], 0.0), axis=2)
    gate_probs = jax.nn.sigmoid(chosen - chosen[:, ::-1])
    kept_mask = slot_ids < CAP
    mix_weight = jnp.where(kept_mask, gate_probs, 0.0)
    slot_hit = slot_ids[:, :, None] == jnp.arange(CAP, dtype=jnp.int32)[None, None, :]
    slot_place = expert_hit[:, :, :, None] & slot_hit[:, :, None, :]
    dispatch = jnp.sum(slot_place.astype(jnp.int32), axis=1).astype(jnp.bfloat16)
    combine_weight = jnp.sum(jnp.where(slot_place, mix_weight[:, :, None, None], 0.0), axis=1)
    outgoing = jnp.einsum(
        "tec,td->ecd", dispatch, row_normed, preferred_element_type=jnp.float32
    ).astype(jnp.bfloat16)
    row_width = outgoing.shape[2]
    local_experts = gate_proj.shape[0]
    expert_groups = EXPERTS // local_experts
    copies = head_count * local_experts // EXPERTS
    outgoing = jnp.broadcast_to(
        outgoing.reshape(expert_groups, 1, local_experts, CAP, row_width),
        (expert_groups, copies, local_experts, CAP, row_width),
    )
    outgoing = outgoing.reshape(head_count, local_experts, CAP, row_width)
    gathered = collect(
        lax.all_to_all(outgoing, HEAD, split_axis=0, concat_axis=0, tiled=True), "state", 3
    )
    partial_out = expert_ffn(gathered, gate_proj, up_proj, down_proj)
    reduced = sum_at_owner(partial_out.astype(jnp.bfloat16), "state", 3)
    returned = lax.all_to_all(
        reduced.astype(jnp.bfloat16), HEAD, split_axis=0, concat_axis=0, tiled=True
    ).astype(reduced.dtype)
    per_expert = returned.reshape(expert_groups, copies, local_experts, CAP, row_width).sum(axis=1)
    per_expert = per_expert.reshape(EXPERTS, CAP, row_width)
    expert_mix = jnp.einsum(
        "tec,ecd->td", combine_weight, per_expert, precision=lax.Precision.HIGHEST
    )
    layer_out = (residual.astype(jnp.float32) + expert_mix).astype(jnp.bfloat16)
    load_own = jnp.sum(jnp.where(expert_hit & kept_mask[:, :, None], 1.0, 0.0), axis=(0, 1)).astype(
        jnp.float32
    )
    prob_own = jnp.sum(jax.nn.sigmoid(logits), axis=0)
    load_sum, prob_sum = (over_axes_2(load_own, HEAD), over_axes_2(prob_own, HEAD))
    total_rows = head_count * own_rows
    aux_value = EXPERTS * jnp.sum(load_sum / (total_rows * TOPK) * (prob_sum / total_rows))
    return (layer_out, new_conv, new_state, load_sum, aux_value.reshape(1))


def solution(mesh):
    finer = Mesh(
        mesh.devices.reshape(mesh.shape["groups"], 32, 2, mesh.shape["state"]),
        ("groups", "head_0", "head_1", "state"),
    )
    in_specs = (
        P(GROUPS_HEAD, "state"),
        P("state"),
        P(None, "state", HEAD),
        P(None, HEAD),
        P(HEAD),
        P(None, "groups", HEAD),
        P(HEAD, None),
        P(),
        P(None, HEAD),
        P(HEAD),
        P("state", HEAD),
        P(HEAD),
        P("state", "groups", HEAD),
        P(HEAD, "state"),
        P(),
        P(),
        P(GROUPS_HEAD, None),
        P(GROUPS_HEAD, None),
        P(HEAD, None, "state"),
        P(HEAD, None, "state"),
        P(HEAD, "state", None),
    )
    out_specs = (
        P(GROUPS_HEAD, "state"),
        P(None, "groups", HEAD),
        P("state", "groups", HEAD),
        P("groups"),
        P("groups"),
    )
    return jax.shard_map(
        per_device, mesh=finer, in_specs=in_specs, out_specs=out_specs, check_vma=False
    )
```

profile of v0, /device:TPU:33, one launch (start us, length us, event | category | flops | bytes accessed | tf_op | source)
XLA Modules:
  0.0 702.4 jit_solution(11900971779136101606)
XLA Ops:
  7.3 0.9 fusion.35
  8.1 9.1 %all_to_all.47 = f32[4,1,4]{2,1,0:T(1,128)S(1)} all-to-all(f32[4,1,4]{2,1,0:T(1,128)S(1)} %broadcast_in_dim.43), channel_id=1, replica_groups=mesh['groups'=2,'head_0'=32,'head_1'=2,'state'=4] {'state'}, dimensions={0} | all-to-all | bytes 128 | tf_op jit(solution)/shard_map/all_to_all | solution.py:25
  17.2 0.7 copy-done.7
  18.0 81.0 %all-gather.2 = bf16[32,4,512]{2,1,0:T(4,128)(2,1)S(1)} all-gather(bf16[1,4,512]{2,1,0:T(4,128)(2,1)S(1)} %fusion.40), channel_id=2, replica_groups=mesh['groups'=2,'head_0'=32,'head_1'=2,'state'=4] {'head_0'}, dimensions={0}, use_global_device_ids=true | all-gather | bytes 135168 | tf_op jit(solution)/shard_map/all_gather | solution.py:43
  99.0 17.9 %all-gather.1 = bf16[64,4,512]{2,1,0:T(4,128)(2,1)S(1)} all-gather(bf16[32,4,512]{2,1,0:T(4,128)(2,1)S(1)} %all-gather.2), channel_id=3, replica_groups=mesh['groups'=2,'head_0'=32,'head_1'=2,'state'=4] {'head_1'}, dimensions={0}, use_global_device_ids=true | all-gather | bytes 393216 | tf_op jit(solution)/shard_map/all_gather | solution.py:43
  117.1 0.9 copy-done.4
  117.9 0.2 convolution_bitcast_fusion
  118.3 17.3 %all_to_all.48 = f32[4,2,256,128]{3,2,1,0:T(8,128)S(1)} all-to-all(f32[4,2,256,128]{3,2,1,0:T(8,128)S(1)} %broadcast_in_dim.45), channel_id=1, replica_groups=mesh['groups'=2,'head_0'=32,'head_1'=2,'state'=4] {'state'}, dimensions={0} | all-to-all | bytes 2097152 | tf_op jit(solution)/shard_map/all_to_all | solution.py:25
  135.7 0.9 copy-done.1
  136.7 0.6 copy-done.11
  137.3 0.8 copy-done.6
  138.2 0.9 fusion.26
  139.2 222.1 %all-reduce.5.cloned.1.call-done = f32[256,288]{0,1:T(8,128)} async-done(((f32[256,288]{0,1:T(8,128)}), f32[256,288]{0,1:T(8,128)}) %all-reduce.5.cloned.1.call-update) | async-done | bytes 294928 | tf_op jit(solution)/shard_map/psum | solution.py:55
  361.4 0.6 copy-done.12
  362.0 75.1 %all-reduce.7.cloned.1.call-done = f32[256,288]{0,1:T(8,128)} async-done(((f32[256,288]{0,1:T(8,128)}), f32[256,288]{0,1:T(8,128)}) %all-reduce.7.cloned.1.call-update) | async-done | bytes 294928 | tf_op jit(solution)/shard_map/psum | solution.py:55
  437.1 1.0 multiply_reduce_fusion.1
  438.1 0.7 dynamic-slice_bitcast_fusion
  438.9 1.3 fusion.52
  440.2 1.1 multiply_reduce_fusion
  441.4 11.7 %all_to_all.49 = f32[4,256,128]{2,1,0:T(8,128)S(1)} all-to-all(f32[4,256,128]{2,1,0:T(8,128)S(1)} %broadcast_in_dim.46), channel_id=1, replica_groups=mesh['groups'=2,'head_0'=32,'head_1'=2,'state'=4] {'state'}, dimensions={0} | all-to-all | bytes 1048576 | tf_op jit(solution)/shard_map/all_to_all | solution.py:25
  453.1 0.6 copy-done.14
  454.0 0.7 copy-done.5
  454.7 0.2 fusion.14
  454.9 1.1 copy.79
  456.0 24.0 %all-to-all-start.3 = ((f32[64,4,512]{2,1,0:T(4,128)}), f32[64,4,512]{2,1,0:T(4,128)S(1)}, u32[]{:S(2)}, u32[]{:S(2)}) async-start(f32[64,4,512]{2,1,0:T(4,128)} %copy.79), calls=%async_computation.3 | async-start | bytes 1048576 | tf_op jit(solution)/shard_map/all_to_all | solution.py:66
  480.1 0.8 dynamic_slice.14
  480.9 0.6 copy-done.9
  481.5 62.5 %all-to-all-done.3 = f32[64,4,512]{2,1,0:T(4,128)S(1)} async-done(((f32[64,4,512]{2,1,0:T(4,128)}), f32[64,4,512]{2,1,0:T(4,128)S(1)}, u32[]{:S(2)}, u32[]{:S(2)}) %all-to-all-start.3) | async-done | bytes 524320 | tf_op jit(solution)/shard_map/all_to_all | solution.py:66
  544.3 0.9 fusion.29
  545.3 0.6 broadcast_in_dim.47
  545.9 3.3 all-to-all-start.4
  549.3 3.9 all-to-all-done.4
  553.5 38.0 %all_to_all.50 = bf16[64,1,2,512]{3,2,1,0:T(2,128)(2,1)S(1)} all-to-all(bf16[64,1,2,512]{3,2,1,0:T(2,128)(2,1)S(1)} %bitcast.106), channel_id=1, replica_groups=mesh['groups'=2,'head_0'=32,'head_1'=2,'state'=4] {'head_0','head_1'}, dimensions={0} | all-to-all | bytes 262144 | tf_op jit(solution)/shard_map/all_to_all | solution.py:195
  591.6 10.9 %all_to_all.51 = bf16[4,64,1,2,512]{4,1,3,2,0:T(8,128)(2,1)S(1)} all-to-all(bf16[4,64,1,2,512]{4,1,3,2,0:T(8,128)(2,1)S(1)} %broadcast_in_dim.60), channel_id=1, replica_groups=mesh['groups'=2,'head_0'=32,'head_1'=2,'state'=4] {'state'}, dimensions={0} | all-to-all | bytes 1048576 | tf_op jit(solution)/shard_map/all_to_all | solution.py:25
  602.5 0.4 copy.83
  602.9 0.4 reshape.169
  603.3 0.4 copy-done.2
  603.7 0.5 convolution_bitcast_fusion.2
  604.2 2.1 convolution_convert_fusion
  606.3 10.1 %all_to_all.52 = bf16[4,64,1,2,512]{4,1,3,2,0:T(8,128)(2,1)S(1)} all-to-all(bf16[4,64,1,2,512]{4,1,3,2,0:T(8,128)(2,1)S(1)} %bitcast.98), channel_id=1, replica_groups=mesh['groups'=2,'head_0'=32,'head_1'=2,'state'=4] {'state'}, dimensions={0} | all-to-all | bytes 1048576 | tf_op jit(solution)/shard_map/all_to_all | solution.py:85
  616.5 0.8 copy.86
  617.3 7.6 %all-to-all-start.8 = ((bf16[64,1,2,512]{3,2,1,0:T(2,128)(2,1)}), bf16[64,1,2,512]{3,2,1,0:T(2,128)(2,1)S(1)}, u32[]{:S(2)}, u32[]{:S(2)}) async-start(bf16[64,1,2,512]{3,2,1,0:T(2,128)(2,1)} %copy.86), calls=%async_computation.8 | async-start | bytes 262144 | tf_op jit(solution)/shard_map/all_to_all | solution.py:199
  624.9 0.8 fusion.12
  626.1 49.9 %all-reduce = (f32[8]{0:T(128)S(1)}, f32[8]{0:T(128)S(1)}) all-reduce(f32[8]{0:T(128)S(1)} %get-tuple-element.5, f32[8]{0:T(128)S(1)} %get-tuple-element.11), channel_id=1, replica_groups=mesh['groups'=2,'head_0'=32,'head_1'=2,'state'=4] {'head_0'}, use_global_device_ids=true, to_apply=%region_18.19 | all-reduce | flops 16 | bytes 128 | tf_op jit(solution)/shard_map/psum | solution.py:55
  676.0 15.6 %all-reduce.1 = (f32[8]{0:T(128)S(1)}, f32[8]{0:T(128)S(1)}) all-reduce(f32[8]{0:T(128)S(1)} %get-tuple-element.7, f32[8]{0:T(128)S(1)} %get-tuple-element.8), channel_id=1, replica_groups=mesh['groups'=2,'head_0'=32,'head_1'=2,'state'=4] {'head_1'}, use_global_device_ids=true, to_apply=%region_19.20 | all-reduce | flops 16 | bytes 128 | tf_op jit(solution)/shard_map/psum | solution.py:55
  691.7 0.5 copy-done.18
  692.1 0.6 multiply_reduce_fusion.2
  693.6 0.8 fusion.4
  (73 shorter events, 2.8 us)
Async XLA Ops:
  7.2 597.0 %copy-start = (bf16[1,224,2048]{2,1,0:T(8,128)(2,1)S(1)}, bf16[1,224,2048]{2,1,0:T(8,128)(2,1)}, u32[]{:S(2)}) copy-start(bf16[1,224,2048]{2,1,0:T(8,128)(2,1)} %param.41) | copy-start | bytes 2752516
  7.2 354.1 %all-reduce.5.cloned.1.call-start = ((), (), s32[]{:S(2)}) async-start(), calls=%async_computation.9 | async-start | bytes 589824 | tf_op jit(solution)/shard_map/psum | solution.py:55
  17.2 0.7 copy-start.7
  17.2 0.7 copy-start.13
  117.0 1.0 copy-start.4
  135.6 1.0 copy-start.1
  135.6 1.0 copy-start.10
  136.6 0.7 copy-start.11
  137.3 0.9 copy-start.6
  139.1 298.0 %all-reduce.7.cloned.1.call-start = ((), (), s32[]{:S(2)}) async-start(), calls=%async_computation.10 | async-start | bytes 589824 | tf_op jit(solution)/shard_map/psum | solution.py:55
  361.3 0.7 copy-start.12
  361.3 77.5 %copy-start.15 = (bf16[256,128]{1,0:T(8,128)(2,1)S(1)}, bf16[256,128]{1,0:T(8,128)(2,1)}, u32[]{:S(2)}) copy-start(bf16[256,128]{1,0:T(8,128)(2,1)} %param.29) | copy-start | bytes 196612
  361.3 77.5 %copy-start.16 = (f32[256]{0:T(256)S(1)}, f32[256]{0:T(256)}, u32[]{:S(2)}) copy-start(f32[256]{0:T(256)} %param.28) | copy-start | bytes 3076
  361.3 77.5 %copy-start.17 = (f32[128]{0:T(128)S(1)}, f32[128]{0:T(128)}, u32[]{:S(2)}) copy-start(f32[128]{0:T(128)} %param.30) | copy-start | bytes 1540
  361.4 78.8 %copy-start.3 = (f32[4,256,128]{2,1,0:T(8,128)S(1)}, f32[4,256,128]{2,1,0:T(8,128)}, u32[]{:S(2)}) copy-start(f32[4,256,128]{2,1,0:T(8,128)} %param.33) | copy-start | bytes 1572868
  453.1 0.7 copy-start.14
  453.8 0.9 copy-start.5
  456.0 88.0 %all-to-all-start.3 = ((f32[64,4,512]{2,1,0:T(4,128)}), f32[64,4,512]{2,1,0:T(4,128)S(1)}, u32[]{:S(2)}, u32[]{:S(2)}) async-start(f32[64,4,512]{2,1,0:T(4,128)} %copy.79), calls=%async_computation.3 | async-start | bytes 1048576 | tf_op jit(solution)/shard_map/all_to_all | solution.py:66
  480.1 0.8 copy-start.8
  480.9 0.7 copy-start.9
  545.9 7.3 %all-to-all-start.4 = ((f32[4,1,36]{2,1,0:T(1,128)}), f32[4,1,36]{2,1,0:T(1,128)S(1)}, u32[]{:S(2)}, u32[]{:S(2)}) async-start(f32[4,1,36]{2,1,0:T(1,128)} %broadcast_in_dim.47), calls=%async_computation.4 | async-start | bytes 4096 | tf_op jit(solution)/shard_map/all_to_all | solution.py:25
  602.5 1.2 copy-start.2
  617.3 76.2 %all-to-all-start.8 = ((bf16[64,1,2,512]{3,2,1,0:T(2,128)(2,1)}), bf16[64,1,2,512]{3,2,1,0:T(2,128)(2,1)S(1)}, u32[]{:S(2)}, u32[]{:S(2)}) async-start(bf16[64,1,2,512]{3,2,1,0:T(2,128)(2,1)} %copy.86), calls=%async_computation.8 | async-start | bytes 262144 | tf_op jit(solution)/shard_map/all_to_all | solution.py:199
  691.6 0.5 copy-start.18
Sparse Core Ops, SparseCore 0:
  139.2 222.0 all-reduce.4
  364.2 72.8 all-reduce.6
where the time goes:
time: 703 us; the launch traced here: 702 us
  waiting for transfers between devices  364 us (52%)
  blocking collectives  262 us (37%)
  starting transfers between devices  35.1 us (5%)
  between operations  16.1 us (2%)
  local copies, waits for them, and re-layouts  13 us (2%)
  matrix products  7.1 us (1%)
    psum x2, waiting for transfers between devices, over_axes_2(): return functools.reduce(lax.psum, axes, shard)  297 us
    all_gather x2, blocking collectives, gather_in_order(): tiles = lax.all_gather(tiles, axes[k])  98.9 us
    psum x2, blocking collectives, over_axes_2(): return functools.reduce(lax.psum, axes, shard)  65.5 us
    all_to_all x1, waiting for transfers between devices, sent_and_summed(): lax.all_to_all(tiles, axis, split_axis=0, concat_axis=0, tiled=True)  62.5 us
    all_to_all x4, blocking collectives, copy_for_each(): lax.all_to_all(jnp.broadcast_to(shard[None], (length, *shard.shape)), axi...  49 us
    all_to_all x1, blocking collectives, per_device(): lax.all_to_all(outgoing, HEAD, split_axis=0, concat_axis=0, tiled=True)  38 us
    all_to_all x1, starting transfers between devices, sent_and_summed(): lax.all_to_all(tiles, axis, split_axis=0, concat_axis=0, tiled=True)  24 us
  transfers between devices with their start and end apart: 5, of which 4 were waited for; matrix products, arithmetic and copies ran while one was open for 0% of the time, Pallas kernels for 0%

commit v1 on v0

v1 whole, which is shorter than its diff:
```python
import functools

import jax
import jax.numpy as jnp
from jax import lax
from jax.experimental import pallas as pl
from jax.experimental.pallas import tpu as pltpu
from jax.sharding import PartitionSpec as P

EXPERTS = 8
TOPK = 2
CAP = 2
LANES = 128
NORM_EPS = 1e-05
STEP_EPS = 1e-06
MESH = pl.DeviceIdType.MESH
F32 = jnp.float32
BF16 = jnp.bfloat16
HI = lax.Precision.HIGHEST


def div(a, n):
    assert n & (n - 1) == 0
    return lax.shift_right_logical(a, jnp.int32(n.bit_length() - 1)) if n > 1 else a


def mod(a, n):
    assert n & (n - 1) == 0
    return a & (n - 1)


def grid_of(rows, cols):
    return (
        lax.broadcasted_iota(jnp.int32, (rows, cols), 0),
        lax.broadcasted_iota(jnp.int32, (rows, cols), 1),
    )


def ones_where(cond, dtype=BF16):
    return jnp.where(cond, 1.0, 0.0).astype(dtype)


def mm(a, b, precision=None):
    return jnp.dot(a, b, preferred_element_type=F32, precision=precision)


def mm_nt(a, b, precision=None):
    return lax.dot_general(
        a, b, (((1,), (1,)), ((), ())), preferred_element_type=F32, precision=precision
    )


def silu(v):
    return v * jax.nn.sigmoid(v)


def softplus(v):
    return jnp.maximum(v, 0.0) + jnp.log1p(jnp.exp(-jnp.abs(v)))


def by_distance(n):
    return sorted(range(1, n), key=lambda k: -min(k, n - k))


STAGES = (
    "tok_far", "tok_near", "branch", "gate", "square", "proj_near", "proj_far", "low_near", "low_state",
    "read", "mix_near", "mix_far", "stat", "row_far", "row_near", "row_state", "out_state", "out_near",
    "out_far", "aux_near", "aux_far",
)
LOADS = ("win", "conv", "sproj", "tproj", "ssm", "oproj", "router", "gate", "up", "down")


def step_kernel(
    n,
    tok_ref, ids_ref, mixn_ref, win_hbm, cw_ref, cb_ref, cs_hbm, sp_hbm, sg_ref, tp_hbm, sb_ref,
    dl_ref, sk_ref, ssm_hbm, op_hbm, mn_ref, rw_hbm, gp_hbm, up_hbm, dn_hbm,
    lo_ref, cin_ref, ns_ref, aux_ref,
    win, cs, sp, tp, ssm, op, rw, gp, up, dn,
    pick, pick_row, G, XC, XG, XS, cob, P2, R2, F2, S2, XR, N3, R3, F3, Q3, ST, F4, G4, rows, rn,
    X5, Y5, N5, R5, F5, Q5, AN, AF,
    send_sem, recv_sem, load_sem,
):
    head = lax.axis_index("head")
    x = lax.axis_index("state")
    b = head // n.NM
    m = head % n.NM
    X, NB, NM, OWN, J, R, T, C, S = n.X, n.NB, n.NM, n.OWN, n.J, n.R, n.T, n.C, n.S

    far = {k: {"head": ((b + k) % NB) * NM + m} for k in range(1, NB)}
    near = {k: {"head": b * NM + (m + k) % NM} for k in range(1, NM)}
    side = {k: {"state": (x + k) % X} for k in range(1, X)}

    barrier = pltpu.get_barrier_semaphore()
    for group in (far, near, side):
        for k in group:
            pl.semaphore_signal(barrier, inc=1, device_id=group[k], device_id_type=MESH)

    loads = {}
    for k, (src, dst) in enumerate(
        (
            (win_hbm, win), (cs_hbm, cs), (sp_hbm, sp), (tp_hbm, tp), (ssm_hbm, ssm), (op_hbm, op),
            (rw_hbm.at[pl.ds(pl.multiple_of(x * n.Q, n.Q), n.Q), :], rw),
            (gp_hbm, gp), (up_hbm, up), (dn_hbm, dn),
        )
    ):
        loads[LOADS[k]] = pltpu.make_async_copy(src, dst, load_sem.at[k])
        loads[LOADS[k]].start()

    pending = []

    def exchange(stage, group, pair):
        at = STAGES.index(stage)
        copies = []
        for k in by_distance(len(group) + 1):
            src, dst = pair(k)
            copy = pltpu.make_async_remote_copy(
                src_ref=src, dst_ref=dst, send_sem=send_sem.at[at, k - 1], recv_sem=recv_sem.at[at, k - 1],
                device_id=group[k], device_id_type=MESH,
            )
            copy.start()
            copies.append(copy)
        pending.extend(copies)
        return copies

    def arrive(copies):
        for copy in copies:
            copy.wait_recv()

    tok_bf = tok_ref[...]
    G[m, b] = tok_bf
    pl.semaphore_wait(barrier, (NB - 1) + (NM - 1) + (X - 1))
    sent = exchange("tok_far", far, lambda k: (tok_ref, G.at[m, b]))

    r_i, c_i = grid_of(T, n.H * R)
    tok_of = (div(mod(c_i, NB * R), R) * NM + div(c_i, NB * R)) * OWN + mod(c_i, OWN)
    match = tok_of == r_i
    which = mod(div(c_i, OWN), J)
    for j in range(J):
        pick[j] = ones_where(match & (which == j))
    r_i, c_i = grid_of(n.SLOTS, n.SLOTS * J)
    match = div(c_i, J * CAP) * CAP + mod(c_i, CAP) == r_i
    which = mod(div(c_i, CAP), J)
    for j in range(J):
        pick_row[j] = ones_where(match & (which == j))

    arrive(sent)
    sent = exchange("tok_near", near, lambda k: (G.at[m], G.at[m]))
    loads["win"].wait()
    arrive(sent)

    gathered = G[...].reshape(n.H * R, LANES)
    conv_part = jnp.zeros((T, C), F32)
    gate_part = jnp.zeros((T, C), F32)
    squares = jnp.zeros((T, 1), F32)
    for j in range(J):
        tok_j = mm(pick[j], gathered)
        squares += jnp.sum(tok_j * tok_j, axis=1, keepdims=True)
        wide = (tok_j * mixn_ref[j : j + 1, :]).astype(BF16)
        conv_part += mm(wide, win[0, j * LANES : (j + 1) * LANES, :])
        gate_part += mm(wide, win[1, j * LANES : (j + 1) * LANES, :])
    XS[x] = jnp.broadcast_to(squares, (T, LANES)).T[:8, :]
    XC[x] = conv_part.astype(BF16)
    sent_sq = exchange("square", side, lambda k: (XS.at[x], XS.at[x]))
    sent = exchange("branch", side, lambda k: (XC.at[x], XC.at[x]))
    XG[x] = gate_part.astype(BF16)
    sent_gate = exchange("gate", side, lambda k: (XG.at[x], XG.at[x]))

    loads["conv"].wait()
    window = cb_ref[...] + sum(cw_ref[k : k + 1, :] * cs[k] for k in range(n.CONV - 1))
    loads["sproj"].wait()
    P2[...] = jnp.zeros_like(P2)
    arrive(sent_sq)
    total = XS[0]
    for k in range(1, X):
        total += XS[k]
    inv_first = lax.rsqrt(jnp.broadcast_to(total[:1, :], (LANES, T)).T[:, :1] / n.D + NORM_EPS)
    arrive(sent)
    conv_in = XC[0].astype(F32)
    for k in range(1, X):
        conv_in += XC[k].astype(F32)
    conv_in = conv_in * inv_first
    cin_ref[...] = conv_in
    conv_out = silu(window + cw_ref[n.CONV - 1 : n.CONV, :] * conv_in)
    cob[...] = conv_out.astype(BF16)

    quarter = T // X
    part = mm(cob[pl.ds(pl.multiple_of(x * quarter, quarter), quarter), :], sp[...])
    P2[:, :, : n.PROJ] = part.reshape(NM, n.TB, n.PROJ)
    R2[m] = P2[m]
    sent = exchange("proj_near", near, lambda k: (P2.at[(m + k) % NM], R2.at[m]))
    arrive(sent)
    total = R2[0]
    for k in range(1, NM):
        total += R2[k]
    F2[b] = total.astype(BF16)
    sent = exchange("proj_far", far, lambda k: (F2.at[b], F2.at[b]))
    for name in ("tproj", "ssm"):
        loads[name].wait()
    arrive(sent)
    total = F2[0].astype(F32)
    for k in range(1, NB):
        total += F2[k].astype(F32)
    S2[x, m] = total.astype(BF16)
    sent = exchange("low_near", near, lambda k: (S2.at[x, m], S2.at[x, m]))
    arrive(sent)
    sent = exchange("low_state", side, lambda k: (S2.at[x], S2.at[x]))
    arrive(sent_gate)
    gate = XG[0].astype(F32)
    for k in range(1, X):
        gate += XG[k].astype(F32)
    gate = silu(gate * inv_first)
    rates = [jnp.exp(dl_ref[k : k + 1, :]) for k in range(S)]
    arrive(sent)

    projected = S2[...].astype(F32).reshape(T, n.PW)
    low = projected[:, : n.RANK]
    step_inv = lax.rsqrt(jnp.mean(low * low, axis=1, keepdims=True) + STEP_EPS)
    step_normed = (low * step_inv * sg_ref[...]).astype(BF16)
    step_size = softplus(mm(step_normed, tp[...]) + sb_ref[...])
    vectors = projected[:, n.RANK :].astype(BF16)
    rows_i, _ = grid_of(LANES, C)
    driven = step_size * conv_out
    read = jnp.zeros((T, C), F32)
    for k in range(S):
        b_in = mm(vectors, ones_where(rows_i == x * S + k))
        c_out = mm(vectors, ones_where(rows_i == n.STATE + x * S + k))
        fresh = jnp.exp(-step_size * rates[k]) * ssm[k] + driven * b_in
        ns_ref[k] = fresh
        read += c_out * fresh
    XR[x] = read.astype(BF16)
    sent = exchange("read", side, lambda k: (XR.at[x], XR.at[x]))
    loads["oproj"].wait()
    r_i, c_i = grid_of(T, T)
    source = (div(mod(r_i, NB * OWN), OWN) * NM + div(r_i, NB * OWN)) * OWN + mod(r_i, OWN)
    by_member = ones_where(source == c_i)
    arrive(sent)
    read = XR[0].astype(F32)
    for k in range(1, X):
        read += XR[k].astype(F32)
    act = ((read + sk_ref[...] * conv_out) * gate).astype(BF16)
    act = mm(by_member, act).astype(BF16)
    N3[...] = mm(act, op[...]).astype(BF16).reshape(NM, NB * OWN, n.Q)
    R3[m] = N3[m]
    sent = exchange("mix_near", near, lambda k: (N3.at[(m + k) % NM], R3.at[m]))
    arrive(sent)
    total = R3[0].astype(F32)
    for k in range(1, NM):
        total += R3[k].astype(F32)
    total = total.astype(BF16)
    r_i, c_i = grid_of(NB * R, NB * OWN)
    match = div(r_i, R) * OWN + mod(r_i, OWN) == c_i
    which = mod(div(r_i, OWN), J)
    spread = jnp.zeros((NB * R, LANES), F32)
    for j in range(J):
        spread += mm(ones_where(match & (which == j)), total[:, j * LANES : (j + 1) * LANES])
    F3[...] = spread.astype(BF16).reshape(NB, R, LANES)
    Q3[b] = F3[b]
    sent = exchange("mix_far", far, lambda k: (F3.at[(b + k) % NB], Q3.at[b]))
    loads["router"].wait()
    arrive(sent)
    total = Q3[0].astype(F32)
    for k in range(1, NB):
        total += Q3[k].astype(F32)

    resid_bf = (tok_bf.astype(F32) + total).astype(BF16)
    resid = resid_bf.astype(F32)
    row_i, lane_i = grid_of(R, LANES)
    hits, kept, slots = [], [], []
    for k in range(TOPK):
        e_k, s_k = ids_ref[:, k : k + 1], ids_ref[:, TOPK + k : TOPK + k + 1]
        keep = s_k < CAP
        hits.append(lane_i == e_k)
        kept.append(keep)
        slots.append((lane_i == e_k * CAP + s_k) & keep)
    dispatch = sum(ones_where(s, F32) for s in slots).astype(BF16)
    d_i, q_i = grid_of(NB * J * CAP, LANES)
    slot_of = ones_where(q_i == div(d_i, J * CAP) * CAP + mod(d_i, CAP))
    d_i, c_i = grid_of(NB * J * CAP, R)
    chosen_rows = jnp.where(
        mod(div(d_i, CAP), J) == div(c_i, OWN), mm_nt(slot_of, dispatch), 0.0
    ).astype(BF16)
    F4[...] = mm(chosen_rows, resid_bf).reshape(NB, J * CAP, LANES).astype(BF16)
    G4[x, m, b] = F4[b]
    sent = exchange("row_far", far, lambda k: (F4.at[(b + k) % NB], G4.at[x, m, b]))

    gain = jnp.zeros((R, LANES), F32)
    for j in range(J):
        gain = jnp.where(div(row_i, OWN) == j, mn_ref[pl.ds(x * J + j, 1), :], gain)
    scaled = resid * gain
    raw = jnp.zeros((R, EXPERTS), F32)
    for j in range(J):
        raw += mm(
            jnp.where(div(row_i, OWN) == j, scaled, 0.0), rw[j * LANES : (j + 1) * LANES, :], HI
        )
    ST[x] = jnp.broadcast_to(jnp.sum(resid * resid, axis=1, keepdims=True), (R, LANES))
    ST[x, :, :EXPERTS] = raw
    sent_stat = exchange("stat", side, lambda k: (ST.at[x], ST.at[x]))
    arrive(sent_stat)
    total = ST[0]
    for k in range(1, X):
        total += ST[k]
    r_i, c_i = grid_of(R, R)
    total = mm(ones_where(mod(r_i, OWN) == mod(c_i, OWN), F32), total, HI)
    inv_second = lax.rsqrt(total[:, EXPERTS : EXPERTS + 1] / n.D + NORM_EPS)
    logits = inv_second * total
    chosen = [jnp.sum(jnp.where(hit, logits, 0.0), axis=1, keepdims=True) for hit in hits]
    mixing = jnp.zeros((R, LANES), F32)
    for k in range(TOPK):
        weight = jax.nn.sigmoid(chosen[k] - chosen[1 - k])
        mixing += jnp.where(slots[k], weight, 0.0)
    first = row_i < OWN
    load = sum(ones_where(hits[k] & kept[k] & first, F32) for k in range(TOPK))
    load = jnp.sum(load, axis=0, keepdims=True)
    prob = jnp.where(first & (lane_i < EXPERTS), jax.nn.sigmoid(logits), 0.0)
    prob = jnp.sum(prob, axis=0, keepdims=True)
    a_i, l_i = grid_of(8, LANES)
    AN[m] = jnp.where(a_i == 0, load, jnp.where(a_i == 1, prob, 0.0))
    sent_aux = exchange("aux_near", near, lambda k: (AN.at[m], AN.at[m]))
    d_i, q_i = grid_of(R, NB * J * CAP)
    combine = jnp.where(
        mod(div(q_i, CAP), J) == div(d_i, OWN), mm_nt(mixing, slot_of.astype(F32), HI), 0.0
    )
    for name in ("gate", "up", "down"):
        loads[name].wait()

    arrive(sent)
    sent = exchange("row_near", near, lambda k: (G4.at[x, m], G4.at[x, m]))
    arrive(sent_aux)
    total = AN[0]
    for k in range(1, NM):
        total += AN[k]
    AF[b] = total
    sent_aux = exchange("aux_far", far, lambda k: (AF.at[b], AF.at[b]))
    arrive(sent)
    sent = exchange("row_state", side, lambda k: (G4.at[x], G4.at[x]))
    arrive(sent)

    squares = jnp.zeros((n.SLOTS, 1), F32)
    for k in range(X):
        source = G4[k].astype(F32).reshape(n.SLOTS * J, LANES).astype(BF16)
        for j in range(J):
            at = k * J + j
            block = mm(pick_row[j], source)
            squares += jnp.sum(block * block, axis=1, keepdims=True)
            rows[:, at * LANES : (at + 1) * LANES] = block * mn_ref[at : at + 1, :]
    inv_rows = lax.rsqrt(squares / n.D + NORM_EPS)
    rn[...] = (rows[...] * inv_rows).astype(BF16)
    normed = rn[...]
    hidden = (silu(mm(normed, gp[0])) * mm(normed, up[0])).astype(BF16)
    for k in range(X):
        X5[k] = mm(hidden, dn[0, :, k * n.Q : (k + 1) * n.Q]).astype(BF16)
    Y5[x] = X5[x]
    sent = exchange("out_state", side, lambda k: (X5.at[(x + k) % X], Y5.at[x]))
    arrive(sent)
    total = Y5[0].astype(F32)
    for k in range(1, X):
        total += Y5[k].astype(F32)
    N5[...] = total.reshape(NM, NB * CAP, n.Q).astype(BF16)
    R5[m] = N5[m]
    sent = exchange("out_near", near, lambda k: (N5.at[(m + k) % NM], R5.at[m]))
    arrive(sent)
    total = R5[0].astype(F32)
    for k in range(1, NM):
        total += R5[k].astype(F32)
    total = total.astype(BF16)
    r_i, c_i = grid_of(NB * J * CAP, NB * CAP)
    match = div(r_i, J * CAP) * CAP + mod(r_i, CAP) == c_i
    which = mod(div(r_i, CAP), J)
    spread = jnp.zeros((NB * J * CAP, LANES), F32)
    for j in range(J):
        spread += mm(ones_where(match & (which == j)), total[:, j * LANES : (j + 1) * LANES])
    F5[...] = spread.reshape(NB, J * CAP, LANES).astype(BF16)
    Q5[b] = F5[b]
    sent = exchange("out_far", far, lambda k: (F5.at[(b + k) % NB], Q5.at[b]))
    arrive(sent_aux)
    total = AF[0]
    for k in range(1, NB):
        total += AF[k]
    share = total[0:1, :] / (T * TOPK) * (total[1:2, :] / T)
    loss = EXPERTS * jnp.sum(jnp.where(l_i[:1] < EXPERTS, share, 0.0), axis=1, keepdims=True)
    aux_ref[...] = jnp.where(a_i == 0, total[0:1, :], loss)
    arrive(sent)
    back = Q5[...].astype(F32).reshape(NB * J * CAP, LANES)
    lo_ref[...] = (resid + mm(combine, back, HI)).astype(BF16)
    for copy in pending:
        copy.wait_send()


class Sizes:
    pass


def per_device(
    head_count, state_count,
    tokens, mixer_norm, input_proj, conv_weight, conv_bias, conv_state, state_proj, step_gain, step_proj,
    step_bias, decay_log, skip_gain, ssm_state, output_proj, moe_norm, router_weight, expert_ids, slot_ids,
    gate_proj, up_proj, down_proj,
):
    n = Sizes()
    n.H, n.X, n.NB = head_count, state_count, EXPERTS
    n.NM = n.H // n.NB
    n.OWN, n.Q = tokens.shape
    n.J = n.Q // LANES
    n.R = n.OWN * n.J
    n.D = n.Q * n.X
    n.CONV = conv_weight.shape[0]
    _, n.T, n.C = conv_state.shape
    n.S = decay_log.shape[0]
    n.STATE = n.S * n.X
    n.RANK, n.PROJ = step_proj.shape[0], state_proj.shape[1]
    n.PW = -(-n.PROJ // LANES) * LANES
    n.TB = n.T // n.X // n.NM
    n.SLOTS = n.NM * n.NB * CAP
    n.FF = gate_proj.shape[2]

    tok = tokens.reshape(n.OWN, n.J, LANES).transpose(1, 0, 2).reshape(n.R, LANES)
    ids = jnp.tile(jnp.concatenate([expert_ids, slot_ids], axis=1), (n.J, 1))
    vm = pl.BlockSpec(memory_space=pltpu.VMEM)
    hbm = pl.BlockSpec(memory_space=pl.ANY)
    V = pltpu.VMEM
    operands = (
        (tok, vm), (ids, vm), (mixer_norm.reshape(n.J, LANES), vm), (input_proj, hbm), (conv_weight, vm),
        (conv_bias.reshape(1, -1), vm), (conv_state, hbm), (state_proj, hbm), (step_gain.reshape(1, -1), vm),
        (step_proj, hbm), (step_bias.reshape(1, -1), vm), (decay_log, vm), (skip_gain.reshape(1, -1), vm),
        (ssm_state, hbm), (output_proj, hbm), (moe_norm.reshape(-1, LANES), vm), (router_weight, hbm),
        (gate_proj, hbm), (up_proj, hbm), (down_proj, hbm),
    )
    wide = n.J * CAP
    scratch = [
        V(input_proj.shape, BF16), V(conv_state.shape, F32), V(state_proj.shape, BF16), V(step_proj.shape, BF16),
        V(ssm_state.shape, F32), V(output_proj.shape, BF16), V((n.Q, EXPERTS), F32), V(gate_proj.shape, BF16),
        V(up_proj.shape, BF16), V(down_proj.shape, BF16),
        V((n.J, n.T, n.H * n.R), BF16),
        V((n.J, n.SLOTS, n.SLOTS * n.J), BF16),
        V((n.NM, n.NB, n.R, LANES), BF16),
        V((n.X, n.T, n.C), BF16), V((n.X, n.T, n.C), BF16),
        V((n.X, 8, n.T), F32),
        V((n.T, n.C), BF16),
        V((n.NM, n.TB, n.PW), F32), V((n.NM, n.TB, n.PW), F32),
        V((n.NB, n.TB, n.PW), BF16), V((n.X, n.NM, n.TB, n.PW), BF16),
        V((n.X, n.T, n.C), BF16),
        V((n.NM, n.NB * n.OWN, n.Q), BF16), V((n.NM, n.NB * n.OWN, n.Q), BF16),
        V((n.NB, n.R, LANES), BF16), V((n.NB, n.R, LANES), BF16),
        V((n.X, n.R, LANES), F32),
        V((n.NB, wide, LANES), BF16), V((n.X, n.NM, n.NB, wide, LANES), BF16),
        V((n.SLOTS, n.D), F32), V((n.SLOTS, n.D), BF16),
        V((n.X, n.SLOTS, n.Q), BF16), V((n.X, n.SLOTS, n.Q), BF16),
        V((n.NM, n.NB * CAP, n.Q), BF16), V((n.NM, n.NB * CAP, n.Q), BF16),
        V((n.NB, wide, LANES), BF16), V((n.NB, wide, LANES), BF16),
        V((n.NM, 8, LANES), F32), V((n.NB, 8, LANES), F32),
    ]
    most = max(n.NM, n.NB, n.X) - 1
    scratch += [
        pltpu.SemaphoreType.DMA((len(STAGES), most)), pltpu.SemaphoreType.DMA((len(STAGES), most)),
        pltpu.SemaphoreType.DMA((len(LOADS),)),
    ]
    out, conv_in, new_state, aux = pl.pallas_call(
        functools.partial(step_kernel, n),
        out_shape=(
            jax.ShapeDtypeStruct((n.R, LANES), BF16),
            jax.ShapeDtypeStruct((n.T, n.C), F32),
            jax.ShapeDtypeStruct(ssm_state.shape, F32),
            jax.ShapeDtypeStruct((8, LANES), F32),
        ),
        in_specs=[spec for _, spec in operands],
        out_specs=(vm, vm, vm, vm),
        scratch_shapes=scratch,
        compiler_params=pltpu.CompilerParams(
            collective_id=0, has_side_effects=True, vmem_limit_bytes=48 * 1024 * 1024
        ),
        name="mixer_moe_step",
    )(*[a for a, _ in operands])
    layer_out = out.reshape(n.J, n.OWN, LANES).transpose(1, 0, 2).reshape(n.OWN, n.Q)
    new_conv = jnp.concatenate([conv_state[1:], conv_in[None]], axis=0)
    return layer_out, new_conv, new_state, aux[0, :EXPERTS], aux[1, :1]


def solution(mesh):
    in_specs = (
        P(("groups", "head"), "state"),
        P("state"),
        P(None, "state", "head"),
        P(None, "head"),
        P("head"),
        P(None, "groups", "head"),
        P("head", None),
        P(),
        P(None, "head"),
        P("head"),
        P("state", "head"),
        P("head"),
        P("state", "groups", "head"),
        P("head", "state"),
        P(),
        P(),
        P(("groups", "head"), None),
        P(("groups", "head"), None),
        P("head", None, "state"),
        P("head", None, "state"),
        P("head", "state", None),
    )
    out_specs = (
        P(("groups", "head"), "state"),
        P(None, "groups", "head"),
        P("state", "groups", "head"),
        P("groups"),
        P("groups"),
    )
    return jax.shard_map(
        functools.partial(per_device, mesh.shape["head"], mesh.shape["state"]),
        mesh=mesh, in_specs=in_specs, out_specs=out_specs, check_vma=False,
    )
```

time: 703 us -> 195 us (0.28)
  waiting for transfers between devices: 364 us -> 0 us
  blocking collectives: 262 us -> 0 us
  Pallas kernels: 0 us -> 180 us
  starting transfers between devices: 35.1 us -> 0 us
  between operations: 16.1 us -> 0.82 us
  matrix products: 7.1 us -> 0 us
    psum x2 -> x0, waiting for transfers between devices: 297 us -> none  [over_axes_2(): return functools.reduce(lax.psum, axes, shard)]
    pallas_call x0 -> x1, Pallas kernels: none -> 180 us  [per_device(): pl.pallas_call(functools.partial(step_kernel, n), out_shape=(jax.ShapeDty...]
    all_gather x2 -> x0, blocking collectives: 98.9 us -> none  [gather_in_order(): tiles = lax.all_gather(tiles, axes[k])]
    all_to_all x6 -> x0, blocking collectives: 97.1 us -> none  [the longest x4 49 us: copy_for_each(): lax.all_to_all(jnp.broadcast_to(shard[None], (length, *shard.shape)), axi...]
    all_to_all x3 -> x0, waiting for transfers between devices: 66.4 us -> none  [the longest x1 62.5 us: sent_and_summed(): lax.all_to_all(tiles, axis, split_axis=0, concat_axis=0, tiled=True)]
    psum x2 -> x0, blocking collectives: 65.5 us -> none  [over_axes_2(): return functools.reduce(lax.psum, axes, shard)]
    all_to_all x3 -> x0, starting transfers between devices: 34.9 us -> none  [the longest x1 24 us: sent_and_summed(): lax.all_to_all(tiles, axis, split_axis=0, concat_axis=0, tiled=True)]
    dot_general x9 -> x0, matrix products: 7.1 us -> none  [the longest x1 2.12 us: expert_ffn(): jnp.einsum('nlcf,lfd->nlcd', hidden, down_proj, preferred_element_type=jn...]
  transfers between devices with their start and end apart: 5 -> 0, of which waited for: 4 -> 0; matrix products, arithmetic and copies ran while one was open for 0% -> 0% of each run, Pallas kernels for 0% -> 0%
where the time goes in v1:
time: 195 us; the launch traced here: 194 us
  Pallas kernels  180 us (92%)
  local copies, waits for them, and re-layouts  13.1 us (7%)
    pallas_call x1, Pallas kernels, per_device(): pl.pallas_call(functools.partial(step_kernel, n), out_shape=(jax.ShapeDty...  180 us
    unnamed x43, local copies, waits for them, and re-layouts  11.1 us

profile of v1, /device:TPU:33, one launch (start us, length us, event | category | flops | bytes accessed | tf_op | source)
XLA Modules:
  0.0 194.3 jit_solution(786731648157062404)
XLA Ops:
  0.6 0.0 copy-start.15
  0.6 1.2 copy.29.rw_hbm
  1.9 0.0 copy-done.15
  1.9 0.5 copy.30.gp_hbm
  2.4 0.0 copy-start
  2.4 0.0 copy-start.1
  2.5 2.3 %copy.31.up_hbm = bf16[1,2048,224]{2,1,0:T(8,128)(2,1)} copy(bf16[1,2048,224]{1,2,0:T(8,128)(2,1)} %param.40) | data formatting | bytes 1835008 | tf_op args[19]
  4.8 0.0 copy-start.16
  4.8 0.0 copy-start.17
  4.8 0.0 copy-start.9
  4.8 0.0 copy-start.10
  4.8 0.0 copy-start.12
  4.8 0.0 copy-start.13
  4.8 0.0 copy-start.14
  4.9 1.1 copy.28.sp_hbm
  5.9 0.0 copy-done.16
  5.9 0.0 copy-done.17
  5.9 0.1 copy.34
  6.0 0.0 copy-start.6
  6.1 0.0 copy-start.7
  6.1 0.0 copy-start.8
  6.1 0.0 copy-start.11
  6.1 0.0 copy-done
  6.1 0.0 copy-done.1
  6.1 0.0 copy-done.9
  6.1 0.0 copy-done.10
  6.1 0.0 copy-done.12
  6.1 0.0 copy-done.13
  6.1 0.0 copy-done.14
  6.1 0.6 copy-done.6
  6.7 0.0 copy-done.7
  6.8 0.0 copy-done.8
  6.8 0.0 copy-done.11
  6.8 0.0 copy-start.2
  6.8 1.0 copy-done.2
  7.8 0.0 copy-start.3
  7.8 0.9 copy-done.3
  8.8 0.0 copy-start.4
  8.8 0.9 copy-done.4
  9.7 0.0 copy-start.5
  9.7 0.8 copy-done.5
  10.5 179.6 %mixer_moe_step.1 = (bf16[16,128]{1,0:T(8,128)(2,1)S(1)}, f32[256,128]{1,0:T(8,128)S(1)}, f32[4,256,128]{2,1,0:T(8,128)S(1)}, f32[8,128]{1,0:T(8,128)S(1)}) custom-call(bf16[16,128]{1,0:T(8,128)(2,1)S(1)} %bitcast.24, s32[16,4]{1,0:T(8,128)S(1)} %bitcast.22, f32[4,128]{1,0:T(4,128)S(1)} %bitcast.26, bf16[2,512,128]{2,1,0:T(8,128)(2,1)S(1)} %copy-done.3, ...), custom_call_target="tpu_custom_call" | custom-call | tf_op jit(solution)/shard_map/mixer_moe_step/pallas_call | solution.py:457
  190.2 0.5 slice.11
  190.7 0.5 slice_bitcast_fusion
  191.2 0.9 slice-done
  192.1 0.8 pad_maximum_fusion
  192.9 0.6 copy.37
  193.5 0.8 copy.38
  (3 shorter events, 0.0 us)
Async XLA Ops:
  0.6 1.3 copy-start.15
  2.4 3.6 %copy-start = (f32[3,256,128]{2,1,0:T(8,128)S(1)}, f32[3,256,128]{2,1,0:T(8,128)}, u32[]{:S(2)}) copy-start(f32[3,256,128]{2,1,0:T(8,128)} %cs_hbm.1) | copy-start | bytes 1179652
  2.4 3.6 %copy-start.1 = (bf16[1,224,2048]{2,1,0:T(8,128)(2,1)S(1)}, bf16[1,224,2048]{2,1,0:T(8,128)(2,1)}, u32[]{:S(2)}) copy-start(bf16[1,224,2048]{2,1,0:T(8,128)(2,1)} %dn_hbm.1) | copy-start | bytes 2752516
  4.8 1.1 copy-start.16
  4.8 1.1 copy-start.17
  4.8 1.3 copy-start.9
  4.8 1.3 copy-start.10
  4.8 1.3 copy-start.12
  4.8 1.3 copy-start.13
  4.8 1.3 copy-start.14
  6.0 0.7 copy-start.6
  6.1 0.7 copy-start.7
  6.1 0.7 copy-start.8
  6.1 0.7 copy-start.11
  6.8 1.0 copy-start.2
  7.8 0.9 copy-start.3
  8.8 0.9 copy-start.4
  9.7 0.8 copy-start.5
  191.2 0.9 slice-start

commit v2 on v1

--- a/solution.py
+++ b/solution.py
@@ -64,47 +64,63 @@
 
 STAGES = (
     "tok_far", "tok_near", "branch", "gate", "square", "proj_near", "proj_far", "low_near", "low_state",
-    "read", "mix_near", "mix_far", "stat", "row_far", "row_near", "row_state", "out_state", "out_near",
+    "read", "mix_near", "mix_far", "stat", "row_far", "row_near", "out_state", "out_near",
     "out_far", "aux_near", "aux_far",
 )
-LOADS = ("win", "conv", "sproj", "tproj", "ssm", "oproj", "router", "gate", "up", "down")
-
-
-def step_kernel(
-    n,
-    tok_ref, ids_ref, mixn_ref, win_hbm, cw_ref, cb_ref, cs_hbm, sp_hbm, sg_ref, tp_hbm, sb_ref,
-    dl_ref, sk_ref, ssm_hbm, op_hbm, mn_ref, rw_hbm, gp_hbm, up_hbm, dn_hbm,
-    lo_ref, cin_ref, ns_ref, aux_ref,
-    win, cs, sp, tp, ssm, op, rw, gp, up, dn,
-    pick, pick_row, G, XC, XG, XS, cob, P2, R2, F2, S2, XR, N3, R3, F3, Q3, ST, F4, G4, rows, rn,
-    X5, Y5, N5, R5, F5, Q5, AN, AF,
-    send_sem, recv_sem, load_sem,
-):
+OPERANDS = (
+    "mixn", "win", "cw", "cb", "sp", "sg", "tp", "sb", "dl", "sk", "ssm", "op", "mn", "eid", "sid", "gp",
+    "up", "dn",
+)
+
+
+def step_kernel(n, tok_hbm, cs_hbm, rw_hbm, *refs):
+    count = len(OPERANDS)
+    sources = refs[:count]
+    lo_ref, nc_ref, ns_ref, load_ref, loss_ref = refs[count : count + 5]
+    held = dict(zip(OPERANDS, refs[count + 5 : 2 * count + 5]))
+    (
+        cs, rw, pick, pick_row, G, XC, XG, XS, cob, P2, R2, F2, S2, XR, N3, R3, F3, Q3, ST, F4, G4, rows,
+        rn, X5, Y5, N5, R5, F5, Q5, AN, AF, send_sem, recv_sem, row_send, row_recv, load_sem,
+    ) = refs[2 * count + 5 :]
     head = lax.axis_index("head")
     x = lax.axis_index("state")
     b = head // n.NM
     m = head % n.NM
     X, NB, NM, OWN, J, R, T, C, S = n.X, n.NB, n.NM, n.OWN, n.J, n.R, n.T, n.C, n.S
 
+    def offset(k):
+        return k if 2 * k <= NM else k - NM
+
     far = {k: {"head": ((b + k) % NB) * NM + m} for k in range(1, NB)}
-    near = {k: {"head": b * NM + (m + k) % NM} for k in range(1, NM)}
+    near = {k: {"head": (head + n.H + offset(k)) % n.H} for k in range(1, NM)}
+    block = {k: {"head": b * NM + (m + k) % NM} for k in range(1, NM)}
     side = {k: {"state": (x + k) % X} for k in range(1, X)}
 
     barrier = pltpu.get_barrier_semaphore()
-    for group in (far, near, side):
+    behind = {k: {"head": (head + n.H - offset(k)) % n.H} for k in near}
+    for group in (side, behind, block, far):
         for k in group:
             pl.semaphore_signal(barrier, inc=1, device_id=group[k], device_id_type=MESH)
 
     loads = {}
-    for k, (src, dst) in enumerate(
-        (
-            (win_hbm, win), (cs_hbm, cs), (sp_hbm, sp), (tp_hbm, tp), (ssm_hbm, ssm), (op_hbm, op),
-            (rw_hbm.at[pl.ds(pl.multiple_of(x * n.Q, n.Q), n.Q), :], rw),
-            (gp_hbm, gp), (up_hbm, up), (dn_hbm, dn),
-        )
-    ):
-        loads[LOADS[k]] = pltpu.make_async_copy(src, dst, load_sem.at[k])
-        loads[LOADS[k]].start()
+
+    def load(name, src, dst):
+        loads[name] = pltpu.make_async_copy(src, dst, load_sem.at[len(loads)])
+        loads[name].start()
+
+    load("tok", tok_hbm, G.at[m, b])
+    for name, src in zip(OPERANDS, sources):
+        load(name, src, held[name])
+    load("conv", cs_hbm.at[0], cs)
+    load("keep", cs_hbm.at[1 : n.CONV - 1], nc_ref.at[0 : n.CONV - 2])
+    load("router", rw_hbm.at[:, pl.ds(pl.multiple_of(x * n.Q, n.Q), n.Q)], rw)
+    mixn_ref, win, cw_ref, cb_ref = held["mixn"], held["win"], held["cw"], held["cb"]
+    sp, sg_ref, tp, sb_ref, dl_ref = held["sp"], held["sg"], held["tp"], held["sb"], held["dl"]
+    sk_ref, ssm, op, mn_ref = held["sk"], held["ssm"], held["op"], held["mn"]
+
+    def loaded(*names):
+        for name in names:
+            loads[name].wait()
 
     pending = []
 
@@ -126,10 +142,10 @@
         for copy in copies:
             copy.wait_recv()
 
-    tok_bf = tok_ref[...]
-    G[m, b] = tok_bf
-    pl.semaphore_wait(barrier, (NB - 1) + (NM - 1) + (X - 1))
-    sent = exchange("tok_far", far, lambda k: (tok_ref, G.at[m, b]))
+    loaded("tok")
+    pl.semaphore_wait(barrier, (NB - 1) + 2 * (NM - 1) + (X - 1))
+    sent = exchange("tok_far", far, lambda k: (G.at[m, b], G.at[m, b]))
+    tok_bf = G[m, b]
 
     r_i, c_i = grid_of(T, n.H * R)
     tok_of = (div(mod(c_i, NB * R), R) * NM + div(c_i, NB * R)) * OWN + mod(c_i, OWN)
@@ -145,7 +161,7 @@
 
     arrive(sent)
     sent = exchange("tok_near", near, lambda k: (G.at[m], G.at[m]))
-    loads["win"].wait()
+    loaded("win", "mixn")
     arrive(sent)
 
     gathered = G[...].reshape(n.H * R, LANES)
@@ -165,9 +181,10 @@
     XG[x] = gate_part.astype(BF16)
     sent_gate = exchange("gate", side, lambda k: (XG.at[x], XG.at[x]))
 
-    loads["conv"].wait()
-    window = cb_ref[...] + sum(cw_ref[k : k + 1, :] * cs[k] for k in range(n.CONV - 1))
-    loads["sproj"].wait()
+    loaded("conv", "keep", "cw", "cb", "sp")
+    window = cb_ref[...] + cw_ref[0:1, :] * cs[...]
+    for k in range(n.CONV - 2):
+        window += cw_ref[k + 1 : k + 2, :] * nc_ref[k]
     P2[...] = jnp.zeros_like(P2)
     arrive(sent_sq)
     total = XS[0]
@@ -179,12 +196,12 @@
     for k in range(1, X):
         conv_in += XC[k].astype(F32)
     conv_in = conv_in * inv_first
-    cin_ref[...] = conv_in
+    nc_ref[n.CONV - 2] = conv_in
     conv_out = silu(window + cw_ref[n.CONV - 1 : n.CONV, :] * conv_in)
     cob[...] = conv_out.astype(BF16)
 
     quarter = T // X
-    part = mm(cob[pl.ds(pl.multiple_of(x * quarter, quarter), quarter), :], sp[...])
+    part = mm_nt(cob[pl.ds(pl.multiple_of(x * quarter, quarter), quarter), :], sp[...])
     P2[:, :, : n.PROJ] = part.reshape(NM, n.TB, n.PROJ)
     R2[m] = P2[m]
     sent = exchange("proj_near", near, lambda k: (P2.at[(m + k) % NM], R2.at[m]))
@@ -194,8 +211,7 @@
         total += R2[k]
     F2[b] = total.astype(BF16)
     sent = exchange("proj_far", far, lambda k: (F2.at[b], F2.at[b]))
-    for name in ("tproj", "ssm"):
-        loads[name].wait()
+    loaded("tp", "ssm", "sg", "sb", "dl")
     arrive(sent)
     total = F2[0].astype(F32)
     for k in range(1, NB):
@@ -229,7 +245,7 @@
         read += c_out * fresh
     XR[x] = read.astype(BF16)
     sent = exchange("read", side, lambda k: (XR.at[x], XR.at[x]))
-    loads["oproj"].wait()
+    loaded("op", "sk")
     r_i, c_i = grid_of(T, T)
     source = (div(mod(r_i, NB * OWN), OWN) * NM + div(r_i, NB * OWN)) * OWN + mod(r_i, OWN)
     by_member = ones_where(source == c_i)
@@ -256,7 +272,7 @@
     F3[...] = spread.astype(BF16).reshape(NB, R, LANES)
     Q3[b] = F3[b]
     sent = exchange("mix_far", far, lambda k: (F3.at[(b + k) % NB], Q3.at[b]))
-    loads["router"].wait()
+    loaded("router", "mn", "eid", "sid")
     arrive(sent)
     total = Q3[0].astype(F32)
     for k in range(1, NB):
@@ -266,8 +282,14 @@
     resid = resid_bf.astype(F32)
     row_i, lane_i = grid_of(R, LANES)
     hits, kept, slots = [], [], []
+    i_i, t_i = grid_of(R, OWN)
+
+    def by_row(ref, k):
+        wide = jnp.broadcast_to(ref[k : k + 1, :], (R, OWN)).astype(F32)
+        return jnp.sum(jnp.where(mod(i_i, OWN) == t_i, wide, 0.0), axis=1, keepdims=True).astype(jnp.int32)
+
     for k in range(TOPK):
-        e_k, s_k = ids_ref[:, k : k + 1], ids_ref[:, TOPK + k : TOPK + k + 1]
+        e_k, s_k = by_row(held["eid"], k), by_row(held["sid"], k)
         keep = s_k < CAP
         hits.append(lane_i == e_k)
         kept.append(keep)
@@ -289,8 +311,8 @@
     scaled = resid * gain
     raw = jnp.zeros((R, EXPERTS), F32)
     for j in range(J):
-        raw += mm(
-            jnp.where(div(row_i, OWN) == j, scaled, 0.0), rw[j * LANES : (j + 1) * LANES, :], HI
+        raw += mm_nt(
+            jnp.where(div(row_i, OWN) == j, scaled, 0.0), rw[:, j * LANES : (j + 1) * LANES], HI
         )
     ST[x] = jnp.broadcast_to(jnp.sum(resid * resid, axis=1, keepdims=True), (R, LANES))
     ST[x, :, :EXPERTS] = raw
@@ -315,49 +337,63 @@
     prob = jnp.sum(prob, axis=0, keepdims=True)
     a_i, l_i = grid_of(8, LANES)
     AN[m] = jnp.where(a_i == 0, load, jnp.where(a_i == 1, prob, 0.0))
-    sent_aux = exchange("aux_near", near, lambda k: (AN.at[m], AN.at[m]))
+    sent_aux = exchange("aux_near", block, lambda k: (AN.at[m], AN.at[m]))
     d_i, q_i = grid_of(R, NB * J * CAP)
     combine = jnp.where(
         mod(div(q_i, CAP), J) == div(d_i, OWN), mm_nt(mixing, slot_of.astype(F32), HI), 0.0
     )
-    for name in ("gate", "up", "down"):
-        loads[name].wait()
-
-    arrive(sent)
-    sent = exchange("row_near", near, lambda k: (G4.at[x, m], G4.at[x, m]))
+    loaded("gp", "up", "dn")
+
+    arrive(sent)
+
+    def to_side(piece, at):
+        copies = []
+        for k in by_distance(X):
+            copy = pltpu.make_async_remote_copy(
+                src_ref=G4.at[x, piece], dst_ref=G4.at[x, piece], send_sem=row_send.at[at, k - 1],
+                recv_sem=row_recv.at[at, k - 1], device_id=side[k], device_id_type=MESH,
+            )
+            copy.start()
+            copies.append(copy)
+        pending.extend(copies)
+        return copies
+
+    sent = exchange("row_near", block, lambda k: (G4.at[x, m], G4.at[x, m]))
+    sideways = to_side(m, 0)
+    for copy, k in reversed(list(zip(sent, by_distance(NM)))):
+        arrive([copy])
+        sideways += to_side((m + NM - k) % NM, k)
     arrive(sent_aux)
     total = AN[0]
     for k in range(1, NM):
         total += AN[k]
     AF[b] = total
     sent_aux = exchange("aux_far", far, lambda k: (AF.at[b], AF.at[b]))
-    arrive(sent)
-    sent = exchange("row_state", side, lambda k: (G4.at[x], G4.at[x]))
-    arrive(sent)
+    arrive(sideways)
 
     squares = jnp.zeros((n.SLOTS, 1), F32)
     for k in range(X):
         source = G4[k].astype(F32).reshape(n.SLOTS * J, LANES).astype(BF16)
         for j in range(J):
             at = k * J + j
-            block = mm(pick_row[j], source)
-            squares += jnp.sum(block * block, axis=1, keepdims=True)
-            rows[:, at * LANES : (at + 1) * LANES] = block * mn_ref[at : at + 1, :]
+            part = mm(pick_row[j], source)
+            squares += jnp.sum(part * part, axis=1, keepdims=True)
+            rows[:, at * LANES : (at + 1) * LANES] = part * mn_ref[at : at + 1, :]
     inv_rows = lax.rsqrt(squares / n.D + NORM_EPS)
     rn[...] = (rows[...] * inv_rows).astype(BF16)
     normed = rn[...]
-    hidden = (silu(mm(normed, gp[0])) * mm(normed, up[0])).astype(BF16)
+    hidden = (silu(mm_nt(normed, held["gp"][0])) * mm_nt(normed, held["up"][0])).astype(BF16)
     for k in range(X):
-        X5[k] = mm(hidden, dn[0, :, k * n.Q : (k + 1) * n.Q]).astype(BF16)
+        X5[k] = mm(hidden, held["dn"][0, :, k * n.Q : (k + 1) * n.Q]).astype(BF16)
+    sent = exchange("out_state", side, lambda k: (X5.at[(x + k) % X], Y5.at[x]))
     Y5[x] = X5[x]
-    sent = exchange("out_state", side, lambda k: (X5.at[(x + k) % X], Y5.at[x]))
     arrive(sent)
     total = Y5[0].astype(F32)
     for k in range(1, X):
         total += Y5[k].astype(F32)
     N5[...] = total.reshape(NM, NB * CAP, n.Q).astype(BF16)
     R5[m] = N5[m]
-    sent = exchange("out_near", near, lambda k: (N5.at[(m + k) % NM], R5.at[m]))
+    sent = exchange("out_near", block, lambda k: (N5.at[(m + k) % NM], R5.at[m]))
     arrive(sent)
     total = R5[0].astype(F32)
     for k in range(1, NM):
@@ -378,12 +414,24 @@
         total += AF[k]
     share = total[0:1, :] / (T * TOPK) * (total[1:2, :] / T)
     loss = EXPERTS * jnp.sum(jnp.where(l_i[:1] < EXPERTS, share, 0.0), axis=1, keepdims=True)
-    aux_ref[...] = jnp.where(a_i == 0, total[0:1, :], loss)
+    load_ref[...] = total[0:1, :EXPERTS]
+    loss_ref[...] = loss
     arrive(sent)
     back = Q5[...].astype(F32).reshape(NB * J * CAP, LANES)
     lo_ref[...] = (resid + mm(combine, back, HI)).astype(BF16)
     for copy in pending:
         copy.wait_send()
+
+
+def finish_kernel(*refs):
+    count = len(refs) // 2
+    copies = [
+        pltpu.make_async_copy(refs[k], refs[count + k], refs[-1].at[k]) for k in range(count)
+    ]
+    for copy in copies:
+        copy.start()
+    for copy in copies:
+        copy.wait()
 
 
 class Sizes:
@@ -414,22 +462,19 @@
     n.FF = gate_proj.shape[2]
 
     tok = tokens.reshape(n.OWN, n.J, LANES).transpose(1, 0, 2).reshape(n.R, LANES)
-    ids = jnp.tile(jnp.concatenate([expert_ids, slot_ids], axis=1), (n.J, 1))
-    vm = pl.BlockSpec(memory_space=pltpu.VMEM)
-    hbm = pl.BlockSpec(memory_space=pl.ANY)
     V = pltpu.VMEM
     operands = (
-        (tok, vm), (ids, vm), (mixer_norm.reshape(n.J, LANES), vm), (input_proj, hbm), (conv_weight, vm),
-        (conv_bias.reshape(1, -1), vm), (conv_state, hbm), (state_proj, hbm), (step_gain.reshape(1, -1), vm),
-        (step_proj, hbm), (step_bias.reshape(1, -1), vm), (decay_log, vm), (skip_gain.reshape(1, -1), vm),
-        (ssm_state, hbm), (output_proj, hbm), (moe_norm.reshape(-1, LANES), vm), (router_weight, hbm),
-        (gate_proj, hbm), (up_proj, hbm), (down_proj, hbm),
-    )
+        mixer_norm.reshape(n.J, LANES), input_proj, conv_weight, conv_bias.reshape(1, -1), state_proj.T,
+        step_gain.reshape(1, -1), step_proj, step_bias.reshape(1, -1), decay_log, skip_gain.reshape(1, -1),
+        ssm_state, output_proj, moe_norm.reshape(-1, LANES), expert_ids.T, slot_ids.T,
+        gate_proj.transpose(0, 2, 1), up_proj.transpose(0, 2, 1), down_proj,
+    )
+    vm = pl.BlockSpec(memory_space=pltpu.VMEM)
+    hbm = pl.BlockSpec(memory_space=pltpu.HBM)
     wide = n.J * CAP
-    scratch = [
-        V(input_proj.shape, BF16), V(conv_state.shape, F32), V(state_proj.shape, BF16), V(step_proj.shape, BF16),
-        V(ssm_state.shape, F32), V(output_proj.shape, BF16), V((n.Q, EXPERTS), F32), V(gate_proj.shape, BF16),
-        V(up_proj.shape, BF16), V(down_proj.shape, BF16),
+    scratch = [V(a.shape, a.dtype) for a in operands]
+    scratch += [
+        V(conv_state.shape[1:], F32), V((EXPERTS, n.Q), F32),
         V((n.J, n.T, n.H * n.R), BF16),
         V((n.J, n.SLOTS, n.SLOTS * n.J), BF16),
         V((n.NM, n.NB, n.R, LANES), BF16),
@@ -450,29 +495,40 @@
         V((n.NM, 8, LANES), F32), V((n.NB, 8, LANES), F32),
     ]
     most = max(n.NM, n.NB, n.X) - 1
+    dma = pltpu.SemaphoreType.DMA
     scratch += [
-        pltpu.SemaphoreType.DMA((len(STAGES), most)), pltpu.SemaphoreType.DMA((len(STAGES), most)),
-        pltpu.SemaphoreType.DMA((len(LOADS),)),
+        dma((len(STAGES), most)), dma((len(STAGES), most)), dma((n.NM, n.X - 1)), dma((n.NM, n.X - 1)),
+        dma((len(OPERANDS) + 4,)),
     ]
-    out, conv_in, new_state, aux = pl.pallas_call(
+    shapes = (
+        jax.ShapeDtypeStruct((n.R, LANES), BF16),
+        jax.ShapeDtypeStruct(conv_state.shape, F32),
+        jax.ShapeDtypeStruct(ssm_state.shape, F32),
+        jax.ShapeDtypeStruct((1, EXPERTS), F32),
+        jax.ShapeDtypeStruct((1, 1), F32),
+    )
+    results = pl.pallas_call(
         functools.partial(step_kernel, n),
-        out_shape=(
-            jax.ShapeDtypeStruct((n.R, LANES), BF16),
-            jax.ShapeDtypeStruct((n.T, n.C), F32),
-            jax.ShapeDtypeStruct(ssm_state.shape, F32),
-            jax.ShapeDtypeStruct((8, LANES), F32),
-        ),
-        in_specs=[spec for _, spec in operands],
-        out_specs=(vm, vm, vm, vm),
+        out_shape=shapes,
+        in_specs=[hbm] * (len(operands) + 3),
+        out_specs=(vm,) * len(shapes),
         scratch_shapes=scratch,
         compiler_params=pltpu.CompilerParams(
             collective_id=0, has_side_effects=True, vmem_limit_bytes=48 * 1024 * 1024
         ),
         name="mixer_moe_step",
-    )(*[a for a, _ in operands])
+    )(*[pltpu.with_memory_space_constraint(a, pltpu.HBM) for a in (tok, conv_state, router_weight.T, *operands)])
+    out, new_conv, new_state, load, loss = pl.pallas_call(
+        finish_kernel,
+        out_shape=shapes,
+        in_specs=[vm] * len(shapes),
+        out_specs=(hbm,) * len(shapes),
+        scratch_shapes=[dma((len(shapes),))],
+        compiler_params=pltpu.CompilerParams(vmem_limit_bytes=1024 * 1024),
+        name="finish",
+    )(*results)
     layer_out = out.reshape(n.J, n.OWN, LANES).transpose(1, 0, 2).reshape(n.OWN, n.Q)
-    new_conv = jnp.concatenate([conv_state[1:], conv_in[None]], axis=0)
-    return layer_out, new_conv, new_state, aux[0, :EXPERTS], aux[1, :1]
+    return layer_out, new_conv, new_state, load.reshape(-1), loss.reshape(1)
 
 
 def solution(mesh):

time: 195 us -> 182 us (0.933)
  local copies, waits for them, and re-layouts: 13.1 us -> 0 us
    unnamed x43 -> x0, local copies, waits for them, and re-layouts: 11.1 us -> none
    pallas_call x1 -> x2, Pallas kernels: 180 us -> 180 us  [the longest x1 178 us: per_device(): pl.pallas_call(functools.partial(step_kernel, n), out_shape=shapes, in_sp...]
where the time goes in v2:
time: 182 us; the launch traced here: 181 us
  Pallas kernels  180 us (99%)
    pallas_call x1, Pallas kernels, per_device(): pl.pallas_call(functools.partial(step_kernel, n), out_shape=shapes, in_sp...  178 us

profile of v2, /device:TPU:33, one launch (start us, length us, event | category | flops | bytes accessed | tf_op | source)
XLA Modules:
  0.0 180.6 jit_solution(1665628867706783147)
XLA Ops:
  0.6 178.4 %mixer_moe_step.1 = (bf16[16,128]{1,0:T(8,128)(2,1)S(1)}, f32[3,256,128]{2,1,0:T(8,128)S(1)}, f32[4,256,128]{2,1,0:T(8,128)S(1)}, f32[1,8]{1,0:T(1,128)S(1)}, f32[1,1]{1,0:T(1,128)}) custom-call(bf16[16,128]{1,0:T(8,128)(2,1)} %bitcast.29, f32[3,256,128]{2,1,0:T(8,128)} %cs_hbm.1, f32[8,2048]{1,0:T(8,128)} %bitcast.27, f32[4,128]{1,0:T(4,128)} %bitcast.30, ...), custom_call_target="tpu_custom_call" | custom-call | tf_op jit(solution)/shard_map/mixer_moe_step/pallas_call | solution.py:510
  179.0 1.6 finish.1

commit v3 on v2

--- a/solution.py
+++ b/solution.py
@@ -63,8 +63,8 @@
 
 
 STAGES = (
-    "tok_far", "tok_near", "branch", "gate", "square", "proj_near", "proj_far", "low_near", "low_state",
-    "read", "mix_near", "mix_far", "stat", "row_far", "row_near", "out_state", "out_near",
+    "tok_near", "tok_last", "branch", "gate", "square", "proj_near", "proj_far", "low_near", "low_state",
+    "read", "mix_near", "mix_far", "stat", "row_far", "row_near", "row_state", "out_state", "out_near",
     "out_far", "aux_near", "aux_far",
 )
 OPERANDS = (
@@ -80,7 +80,8 @@
     held = dict(zip(OPERANDS, refs[count + 5 : 2 * count + 5]))
     (
         cs, rw, pick, pick_row, G, XC, XG, XS, cob, P2, R2, F2, S2, XR, N3, R3, F3, Q3, ST, F4, G4, rows,
-        rn, X5, Y5, N5, R5, F5, Q5, AN, AF, send_sem, recv_sem, row_send, row_recv, load_sem,
+        rn, X5, Y5, N5, R5, F5, Q5, AN, AF, send_sem, recv_sem, piece_sem, up_send, up_recv, down_send,
+        down_recv, ready_up, ready_near, load_sem,
     ) = refs[2 * count + 5 :]
     head = lax.axis_index("head")
     x = lax.axis_index("state")
@@ -97,10 +98,20 @@
     side = {k: {"state": (x + k) % X} for k in range(1, X)}
 
     barrier = pltpu.get_barrier_semaphore()
-    behind = {k: {"head": (head + n.H - offset(k)) % n.H} for k in near}
-    for group in (side, behind, block, far):
-        for k in group:
-            pl.semaphore_signal(barrier, inc=1, device_id=group[k], device_id_type=MESH)
+    around = [(head + n.H + o) % n.H for o in range(-(NM // 2), NM // 2 + 1) if o]
+
+    def greet(partner):
+        pl.semaphore_signal(barrier, inc=1, device_id=partner, device_id_type=MESH)
+
+    for k in side:
+        greet(side[k])
+    for other in around:
+        pl.when(other > head)(functools.partial(greet, {"head": other}))
+    for k in range(1, NB):
+        pl.when(b + k < NB)(functools.partial(greet, {"head": (b + k) * NM + m}))
+    expected = b + (X - 1)
+    for other in around:
+        expected += jnp.where(other < head, 1, 0)
 
     loads = {}
 
@@ -124,27 +135,99 @@
 
     pending = []
 
-    def exchange(stage, group, pair):
+    def remote(src, dst, send, recv, partner):
+        return pltpu.make_async_remote_copy(
+            src_ref=src, dst_ref=dst, send_sem=send, recv_sem=recv, device_id=partner, device_id_type=MESH
+        )
+
+    def exchange(stage, group, pair, landing, first=None):
         at = STAGES.index(stage)
-        copies = []
         for k in by_distance(len(group) + 1):
+            if first is not None:
+                first(k)
             src, dst = pair(k)
-            copy = pltpu.make_async_remote_copy(
-                src_ref=src, dst_ref=dst, send_sem=send_sem.at[at, k - 1], recv_sem=recv_sem.at[at, k - 1],
-                device_id=group[k], device_id_type=MESH,
+            remote(src, dst, send_sem.at[at], recv_sem.at[at], group[k]).start()
+        pending.append(pltpu.make_async_copy(landing, landing, send_sem.at[at]))
+        return pltpu.make_async_copy(landing, landing, recv_sem.at[at])
+
+    def arrive(copy):
+        copy.wait()
+
+    def by_pieces(name, group, ref, at):
+        near_at, side_at = STAGES.index(name + "_near"), STAGES.index(name + "_state")
+        sent = {}
+        order = by_distance(NM)
+        for k in order:
+            sent[k] = remote(
+                ref.at[x, m], ref.at[x, m], send_sem.at[near_at], piece_sem.at[at, k - 1], group[k]
             )
-            copy.start()
-            copies.append(copy)
-        pending.extend(copies)
-        return copies
-
-    def arrive(copies):
-        for copy in copies:
-            copy.wait_recv()
+            sent[k].start()
+        for step in [0] + order[::-1]:
+            piece = (m + NM - step) % NM
+            if step:
+                sent[step].wait_recv()
+            for k in by_distance(X):
+                remote(
+                    ref.at[x, piece], ref.at[x, piece], send_sem.at[side_at], recv_sem.at[side_at], side[k]
+                ).start()
+        landing = ref.at[0, 0 : NM - 1]
+        pending.append(pltpu.make_async_copy(landing, landing, send_sem.at[near_at]))
+        landing = ref.at[0 : X - 1]
+        pending.append(pltpu.make_async_copy(landing, landing, send_sem.at[side_at]))
+        return pltpu.make_async_copy(landing, landing, recv_sem.at[side_at])
 
     loaded("tok")
-    pl.semaphore_wait(barrier, (NB - 1) + 2 * (NM - 1) + (X - 1))
-    sent = exchange("tok_far", far, lambda k: (G.at[m, b], G.at[m, b]))
+    pl.semaphore_wait(barrier, expected)
+
+    @pl.when(b > 0)
+    def _():
+        pl.semaphore_signal(ready_up, inc=1, device_id={"head": head - NM}, device_id_type=MESH)
+
+    for k in near:
+        source = (head + n.H - offset(k)) % n.H
+
+        @pl.when(source < head)
+        def _(k=k, source=source):
+            pl.semaphore_signal(
+                ready_near.at[k - 1], inc=1, device_id={"head": source}, device_id_type=MESH
+            )
+
+    own = G.at[m, b]
+    downs = []
+    for k in by_distance(NB):
+        copy = remote(own, own, down_send.at[k - 1], down_recv.at[k - 1], {"head": head - k * NM})
+        pl.when(b >= k)(copy.start)
+        downs.append((k, copy))
+    climbing = b < NB - 1
+    ups = [
+        remote(G.at[m, k], G.at[m, k], up_send.at[k], up_recv.at[k], {"head": head + NM})
+        for k in range(NB - 1)
+    ]
+
+    @pl.when(climbing)
+    def _():
+        pl.semaphore_wait(ready_up, 1)
+
+    for k in range(NB - 2, -1, -1):
+        pl.when(k < b)(ups[k].wait_recv)
+        pl.when((k <= b) & climbing)(ups[k].start)
+
+    def from_above(last):
+        for k, copy in sorted(downs, key=lambda t: t[0]):
+            pl.when((b + k == NB - 1) if last else (b + k < NB - 1))(copy.wait_recv)
+
+    def near_ready(k):
+        target = (head + n.H + offset(k)) % n.H
+
+        @pl.when(target > head)
+        def _():
+            pl.semaphore_wait(ready_near.at[k - 1], 1)
+
+    from_above(False)
+    early = G.at[m, 0 : NB - 1]
+    sent_early = exchange(
+        "tok_near", near, lambda k: (early, early), G.at[0 : NM - 1, 0 : NB - 1], near_ready
+    )
     tok_bf = G[m, b]
 
     r_i, c_i = grid_of(T, n.H * R)
@@ -159,9 +242,11 @@
     for j in range(J):
         pick_row[j] = ones_where(match & (which == j))
 
-    arrive(sent)
-    sent = exchange("tok_near", near, lambda k: (G.at[m], G.at[m]))
+    from_above(True)
+    final = G.at[m, NB - 1]
+    sent = exchange("tok_last", near, lambda k: (final, final), G.at[0, 0 : NM - 1])
     loaded("win", "mixn")
+    arrive(sent_early)
     arrive(sent)
 
     gathered = G[...].reshape(n.H * R, LANES)
@@ -171,15 +256,17 @@
     for j in range(J):
         tok_j = mm(pick[j], gathered)
         squares += jnp.sum(tok_j * tok_j, axis=1, keepdims=True)
-        wide = (tok_j * mixn_ref[j : j + 1, :]).astype(BF16)
-        conv_part += mm(wide, win[0, j * LANES : (j + 1) * LANES, :])
-        gate_part += mm(wide, win[1, j * LANES : (j + 1) * LANES, :])
+        wide = tok_j * mixn_ref[j : j + 1, :]
+        high = wide.astype(BF16)
+        for half in (high, (wide - high.astype(F32)).astype(BF16)):
+            conv_part += mm(half, win[0, j * LANES : (j + 1) * LANES, :])
+            gate_part += mm(half, win[1, j * LANES : (j + 1) * LANES, :])
     XS[x] = jnp.broadcast_to(squares, (T, LANES)).T[:8, :]
     XC[x] = conv_part.astype(BF16)
-    sent_sq = exchange("square", side, lambda k: (XS.at[x], XS.at[x]))
-    sent = exchange("branch", side, lambda k: (XC.at[x], XC.at[x]))
+    sent_sq = exchange("square", side, lambda k: (XS.at[x], XS.at[x]), XS.at[0 : X - 1])
+    sent = exchange("branch", side, lambda k: (XC.at[x], XC.at[x]), XC.at[0 : X - 1])
     XG[x] = gate_part.astype(BF16)
-    sent_gate = exchange("gate", side, lambda k: (XG.at[x], XG.at[x]))
+    sent_gate = exchange("gate", side, lambda k: (XG.at[x], XG.at[x]), XG.at[0 : X - 1])
 
     loaded("conv", "keep", "cw", "cb", "sp")
     window = cb_ref[...] + cw_ref[0:1, :] * cs[...]
@@ -201,63 +288,73 @@
     cob[...] = conv_out.astype(BF16)
 
     quarter = T // X
+    spare = n.PROJ - n.RANK
+
+    def in_halves(wide):
+        low, vectors = wide[:, : n.RANK], wide[:, n.RANK :]
+        high = vectors.astype(BF16).astype(F32)
+        rest = pltpu.roll(vectors - high, spare, 1)
+        return jnp.concatenate([low, high + rest], axis=1).astype(BF16)
+
     part = mm_nt(cob[pl.ds(pl.multiple_of(x * quarter, quarter), quarter), :], sp[...])
     P2[:, :, : n.PROJ] = part.reshape(NM, n.TB, n.PROJ)
     R2[m] = P2[m]
-    sent = exchange("proj_near", near, lambda k: (P2.at[(m + k) % NM], R2.at[m]))
+    sent = exchange("proj_near", near, lambda k: (P2.at[(m + k) % NM], R2.at[m]), R2.at[0 : NM - 1])
     arrive(sent)
     total = R2[0]
     for k in range(1, NM):
         total += R2[k]
-    F2[b] = total.astype(BF16)
-    sent = exchange("proj_far", far, lambda k: (F2.at[b], F2.at[b]))
+    F2[b] = in_halves(total)
+    sent = exchange("proj_far", far, lambda k: (F2.at[b], F2.at[b]), F2.at[0 : NB - 1])
     loaded("tp", "ssm", "sg", "sb", "dl")
     arrive(sent)
     total = F2[0].astype(F32)
     for k in range(1, NB):
         total += F2[k].astype(F32)
-    S2[x, m] = total.astype(BF16)
-    sent = exchange("low_near", near, lambda k: (S2.at[x, m], S2.at[x, m]))
-    arrive(sent)
-    sent = exchange("low_state", side, lambda k: (S2.at[x], S2.at[x]))
+    low, vectors = total[:, : n.RANK], total[:, n.RANK :]
+    step_inv = lax.rsqrt(jnp.mean(low * low, axis=1, keepdims=True) + STEP_EPS)
+    vectors = vectors + pltpu.roll(vectors, LANES - spare, 1)
+    _, l_i = grid_of(n.TB, LANES)
+    vectors = jnp.where(l_i < spare, vectors, 0.0)
+    S2[x, m] = in_halves(jnp.concatenate([low * step_inv * sg_ref[...], vectors], axis=1))
+    sent = by_pieces("low", near, S2, 0)
     arrive(sent_gate)
-    gate = XG[0].astype(F32)
+    gate = gate_part
     for k in range(1, X):
-        gate += XG[k].astype(F32)
+        gate += XG[(x + k) % X].astype(F32)
     gate = silu(gate * inv_first)
     rates = [jnp.exp(dl_ref[k : k + 1, :]) for k in range(S)]
     arrive(sent)
 
     projected = S2[...].astype(F32).reshape(T, n.PW)
-    low = projected[:, : n.RANK]
-    step_inv = lax.rsqrt(jnp.mean(low * low, axis=1, keepdims=True) + STEP_EPS)
-    step_normed = (low * step_inv * sg_ref[...]).astype(BF16)
+    step_normed = projected[:, : n.RANK].astype(BF16)
     step_size = softplus(mm(step_normed, tp[...]) + sb_ref[...])
     vectors = projected[:, n.RANK :].astype(BF16)
     rows_i, _ = grid_of(LANES, C)
     driven = step_size * conv_out
     read = jnp.zeros((T, C), F32)
     for k in range(S):
-        b_in = mm(vectors, ones_where(rows_i == x * S + k))
-        c_out = mm(vectors, ones_where(rows_i == n.STATE + x * S + k))
+        at = x * S + k
+        b_in = mm(vectors, ones_where((rows_i == at) | (rows_i == spare + at)))
+        at = at + n.STATE
+        c_out = mm(vectors, ones_where((rows_i == at) | (rows_i == spare + at)))
         fresh = jnp.exp(-step_size * rates[k]) * ssm[k] + driven * b_in
         ns_ref[k] = fresh
         read += c_out * fresh
     XR[x] = read.astype(BF16)
-    sent = exchange("read", side, lambda k: (XR.at[x], XR.at[x]))
+    sent = exchange("read", side, lambda k: (XR.at[x], XR.at[x]), XR.at[0 : X - 1])
     loaded("op", "sk")
     r_i, c_i = grid_of(T, T)
     source = (div(mod(r_i, NB * OWN), OWN) * NM + div(r_i, NB * OWN)) * OWN + mod(r_i, OWN)
     by_member = ones_where(source == c_i)
     arrive(sent)
-    read = XR[0].astype(F32)
     for k in range(1, X):
-        read += XR[k].astype(F32)
+        read += XR[(x + k) % X].astype(F32)
     act = ((read + sk_ref[...] * conv_out) * gate).astype(BF16)
     act = mm(by_member, act).astype(BF16)
     N3[...] = mm(act, op[...]).astype(BF16).reshape(NM, NB * OWN, n.Q)
     R3[m] = N3[m]
-    sent = exchange("mix_near", near, lambda k: (N3.at[(m + k) % NM], R3.at[m]))
+    sent = exchange("mix_near", near, lambda k: (N3.at[(m + k) % NM], R3.at[m]), R3.at[0 : NM - 1])
     arrive(sent)
     total = R3[0].astype(F32)
     for k in range(1, NM):
@@ -271,7 +368,7 @@
         spread += mm(ones_where(match & (which == j)), total[:, j * LANES : (j + 1) * LANES])
     F3[...] = spread.astype(BF16).reshape(NB, R, LANES)
     Q3[b] = F3[b]
-    sent = exchange("mix_far", far, lambda k: (F3.at[(b + k) % NB], Q3.at[b]))
+    sent = exchange("mix_far", far, lambda k: (F3.at[(b + k) % NB], Q3.at[b]), Q3.at[0 : NB - 1])
     loaded("router", "mn", "eid", "sid")
     arrive(sent)
     total = Q3[0].astype(F32)
@@ -303,7 +400,9 @@
     ).astype(BF16)
     F4[...] = mm(chosen_rows, resid_bf).reshape(NB, J * CAP, LANES).astype(BF16)
     G4[x, m, b] = F4[b]
-    sent = exchange("row_far", far, lambda k: (F4.at[(b + k) % NB], G4.at[x, m, b]))
+    sent = exchange(
+        "row_far", far, lambda k: (F4.at[(b + k) % NB], G4.at[x, m, b]), G4.at[x, m, 0 : NB - 1]
+    )
 
     gain = jnp.zeros((R, LANES), F32)
     for j in range(J):
@@ -316,7 +415,7 @@
         )
     ST[x] = jnp.broadcast_to(jnp.sum(resid * resid, axis=1, keepdims=True), (R, LANES))
     ST[x, :, :EXPERTS] = raw
-    sent_stat = exchange("stat", side, lambda k: (ST.at[x], ST.at[x]))
+    sent_stat = exchange("stat", side, lambda k: (ST.at[x], ST.at[x]), ST.at[0 : X - 1])
     arrive(sent_stat)
     total = ST[0]
     for k in range(1, X):
@@ -337,7 +436,7 @@
     prob = jnp.sum(prob, axis=0, keepdims=True)
     a_i, l_i = grid_of(8, LANES)
     AN[m] = jnp.where(a_i == 0, load, jnp.where(a_i == 1, prob, 0.0))
-    sent_aux = exchange("aux_near", block, lambda k: (AN.at[m], AN.at[m]))
+    sent_aux = exchange("aux_near", block, lambda k: (AN.at[m], AN.at[m]), AN.at[0 : NM - 1])
     d_i, q_i = grid_of(R, NB * J * CAP)
     combine = jnp.where(
         mod(div(q_i, CAP), J) == div(d_i, OWN), mm_nt(mixing, slot_of.astype(F32), HI), 0.0
@@ -346,29 +445,13 @@
 
     arrive(sent)
 
-    def to_side(piece, at):
-        copies = []
-        for k in by_distance(X):
-            copy = pltpu.make_async_remote_copy(
-                src_ref=G4.at[x, piece], dst_ref=G4.at[x, piece], send_sem=row_send.at[at, k - 1],
-                recv_sem=row_recv.at[at, k - 1], device_id=side[k], device_id_type=MESH,
-            )
-            copy.start()
-            copies.append(copy)
-        pending.extend(copies)
-        return copies
-
-    sent = exchange("row_near", block, lambda k: (G4.at[x, m], G4.at[x, m]))
-    sideways = to_side(m, 0)
-    for copy, k in reversed(list(zip(sent, by_distance(NM)))):
-        arrive([copy])
-        sideways += to_side((m + NM - k) % NM, k)
+    sideways = by_pieces("row", block, G4, 1)
     arrive(sent_aux)
     total = AN[0]
     for k in range(1, NM):
         total += AN[k]
     AF[b] = total
-    sent_aux = exchange("aux_far", far, lambda k: (AF.at[b], AF.at[b]))
+    sent_aux = exchange("aux_far", far, lambda k: (AF.at[b], AF.at[b]), AF.at[0 : NB - 1])
     arrive(sideways)
 
     squares = jnp.zeros((n.SLOTS, 1), F32)
@@ -385,7 +468,7 @@
     hidden = (silu(mm_nt(normed, held["gp"][0])) * mm_nt(normed, held["up"][0])).astype(BF16)
     for k in range(X):
         X5[k] = mm(hidden, held["dn"][0, :, k * n.Q : (k + 1) * n.Q]).astype(BF16)
-    sent = exchange("out_state", side, lambda k: (X5.at[(x + k) % X], Y5.at[x]))
+    sent = exchange("out_state", side, lambda k: (X5.at[(x + k) % X], Y5.at[x]), Y5.at[0 : X - 1])
     Y5[x] = X5[x]
     arrive(sent)
     total = Y5[0].astype(F32)
@@ -393,7 +476,7 @@
         total += Y5[k].astype(F32)
     N5[...] = total.reshape(NM, NB * CAP, n.Q).astype(BF16)
     R5[m] = N5[m]
-    sent = exchange("out_near", block, lambda k: (N5.at[(m + k) % NM], R5.at[m]))
+    sent = exchange("out_near", block, lambda k: (N5.at[(m + k) % NM], R5.at[m]), R5.at[0 : NM - 1])
     arrive(sent)
     total = R5[0].astype(F32)
     for k in range(1, NM):
@@ -407,7 +490,7 @@
         spread += mm(ones_where(match & (which == j)), total[:, j * LANES : (j + 1) * LANES])
     F5[...] = spread.reshape(NB, J * CAP, LANES).astype(BF16)
     Q5[b] = F5[b]
-    sent = exchange("out_far", far, lambda k: (F5.at[(b + k) % NB], Q5.at[b]))
+    sent = exchange("out_far", far, lambda k: (F5.at[(b + k) % NB], Q5.at[b]), Q5.at[0 : NB - 1])
     arrive(sent_aux)
     total = AF[0]
     for k in range(1, NB):
@@ -420,7 +503,11 @@
     back = Q5[...].astype(F32).reshape(NB * J * CAP, LANES)
     lo_ref[...] = (resid + mm(combine, back, HI)).astype(BF16)
     for copy in pending:
-        copy.wait_send()
+        copy.wait()
+    for k, copy in downs:
+        pl.when(b >= k)(copy.wait_send)
+    for k in range(NB - 1):
+        pl.when((k <= b) & climbing)(ups[k].wait_send)
 
 
 def finish_kernel(*refs):
@@ -494,11 +581,11 @@
         V((n.NB, wide, LANES), BF16), V((n.NB, wide, LANES), BF16),
         V((n.NM, 8, LANES), F32), V((n.NB, 8, LANES), F32),
     ]
-    most = max(n.NM, n.NB, n.X) - 1
-    dma = pltpu.SemaphoreType.DMA
+    dma, regular = pltpu.SemaphoreType.DMA, pltpu.SemaphoreType.REGULAR
+    climb = dma((n.NB - 1,))
     scratch += [
-        dma((len(STAGES), most)), dma((len(STAGES), most)), dma((n.NM, n.X - 1)), dma((n.NM, n.X - 1)),
-        dma((len(OPERANDS) + 4,)),
+        dma((len(STAGES),)), dma((len(STAGES),)), dma((2, n.NM - 1)), climb, climb, climb, climb,
+        regular, regular((n.NM - 1,)), dma((len(OPERANDS) + 4,)),
     ]
     shapes = (
         jax.ShapeDtypeStruct((n.R, LANES), BF16),

time: 182 us -> 189 us (1.038)
  Pallas kernels: 180 us -> 188 us
    pallas_call x1, Pallas kernels: 178 us -> 187 us  [per_device(): pl.pallas_call(functools.partial(step_kernel, n), out_shape=shapes, in_sp...]
where the time goes in v3:
time: 189 us
  Pallas kernels  188 us (99%)
    pallas_call x1, Pallas kernels, per_device(): pl.pallas_call(functools.partial(step_kernel, n), out_shape=shapes, in_sp...  187 us

profile of v3, /device:TPU:33, one launch (start us, length us, event | category | flops | bytes accessed | tf_op | source)
XLA Modules:
  0.0 188.9 jit_solution(12920674389577900824)
XLA Ops:
  0.6 186.6 %mixer_moe_step.1 = (bf16[16,128]{1,0:T(8,128)(2,1)S(1)}, f32[3,256,128]{2,1,0:T(8,128)S(1)}, f32[4,256,128]{2,1,0:T(8,128)S(1)}, f32[1,8]{1,0:T(1,128)S(1)}, f32[1,1]{1,0:T(1,128)}) custom-call(bf16[16,128]{1,0:T(8,128)(2,1)} %bitcast.29, f32[3,256,128]{2,1,0:T(8,128)} %cs_hbm.1, f32[8,2048]{1,0:T(8,128)} %bitcast.27, f32[4,128]{1,0:T(4,128)} %bitcast.30, ...), custom_call_target="tpu_custom_call" | custom-call | tf_op jit(solution)/shard_map/mixer_moe_step/pallas_call | solution.py:597
  187.3 1.6 finish.1

commit v4 on v3

--- a/solution.py
+++ b/solution.py
@@ -81,7 +81,7 @@
     (
         cs, rw, pick, pick_row, G, XC, XG, XS, cob, P2, R2, F2, S2, XR, N3, R3, F3, Q3, ST, F4, G4, rows,
         rn, X5, Y5, N5, R5, F5, Q5, AN, AF, send_sem, recv_sem, piece_sem, up_send, up_recv, down_send,
-        down_recv, ready_up, ready_near, load_sem,
+        down_recv, wrap_sem, ready_up, ready_wrap, ready_near, load_sem,
     ) = refs[2 * count + 5 :]
     head = lax.axis_index("head")
     x = lax.axis_index("state")
@@ -208,9 +208,33 @@
     def _():
         pl.semaphore_wait(ready_up, 1)
 
-    for k in range(NB - 2, -1, -1):
+    top = NB - 1
+    around_top = remote(G.at[m, 0], G.at[m, 0], wrap_sem.at[0], wrap_sem.at[1], {"head": top * NM + m})
+    descent = remote(G.at[m, 0], G.at[m, 0], wrap_sem.at[0], wrap_sem.at[1], {"head": head - NM})
+    below = b < NB // 2
+
+    @pl.when(b == top)
+    def _():
+        pl.semaphore_signal(ready_wrap, inc=1, device_id={"head": m}, device_id_type=MESH)
+        around_top.wait_recv()
+        if top > NB // 2 + 1:
+            descent.start()
+
+    for k in range(NB - 2, 0, -1):
         pl.when(k < b)(ups[k].wait_recv)
         pl.when((k <= b) & climbing)(ups[k].start)
+    pl.when((b > 0) & (b <= NB // 2))(ups[0].wait_recv)
+    pl.when(below)(ups[0].start)
+
+    @pl.when(b == 0)
+    def _():
+        pl.semaphore_wait(ready_wrap, 1)
+        around_top.start()
+
+    @pl.when((b > NB // 2) & (b < top))
+    def _():
+        around_top.wait_recv()
+        pl.when(b > NB // 2 + 1)(descent.start)
 
     def from_above(last):
         for k, copy in sorted(downs, key=lambda t: t[0]):
@@ -466,9 +490,14 @@
     rn[...] = (rows[...] * inv_rows).astype(BF16)
     normed = rn[...]
     hidden = (silu(mm_nt(normed, held["gp"][0])) * mm_nt(normed, held["up"][0])).astype(BF16)
-    for k in range(X):
-        X5[k] = mm(hidden, held["dn"][0, :, k * n.Q : (k + 1) * n.Q]).astype(BF16)
-    sent = exchange("out_state", side, lambda k: (X5.at[(x + k) % X], Y5.at[x]), Y5.at[0 : X - 1])
+
+    def down_part(k):
+        at = (x + k) % X
+        columns = pl.ds(pl.multiple_of(at * n.Q, n.Q), n.Q)
+        X5[at] = mm(hidden, held["dn"][0, :, columns]).astype(BF16)
+
+    sent = exchange("out_state", side, lambda k: (X5.at[(x + k) % X], Y5.at[x]), Y5.at[0 : X - 1], down_part)
+    down_part(0)
     Y5[x] = X5[x]
     arrive(sent)
     total = Y5[0].astype(F32)
@@ -506,8 +535,10 @@
         copy.wait()
     for k, copy in downs:
         pl.when(b >= k)(copy.wait_send)
-    for k in range(NB - 1):
+    for k in range(1, NB - 1):
         pl.when((k <= b) & climbing)(ups[k].wait_send)
+    pl.when(below)(ups[0].wait_send)
+    pl.when((b == 0) | (b > NB // 2 + 1))(around_top.wait_send)
 
 
 def finish_kernel(*refs):
@@ -585,7 +616,7 @@
     climb = dma((n.NB - 1,))
     scratch += [
         dma((len(STAGES),)), dma((len(STAGES),)), dma((2, n.NM - 1)), climb, climb, climb, climb,
-        regular, regular((n.NM - 1,)), dma((len(OPERANDS) + 4,)),
+        dma((2,)), regular, regular, regular((n.NM - 1,)), dma((len(OPERANDS) + 4,)),
     ]
     shapes = (
         jax.ShapeDtypeStruct((n.R, LANES), BF16),

time: 189 us -> 187 us (0.989)
  Pallas kernels: 188 us -> 186 us
    pallas_call x1, Pallas kernels: 187 us -> 184 us  [per_device(): pl.pallas_call(functools.partial(step_kernel, n), out_shape=shapes, in_sp...]
where the time goes in v4:
time: 187 us; the launch traced here: 186 us
  Pallas kernels  186 us (99%)
    pallas_call x1, Pallas kernels, per_device(): pl.pallas_call(functools.partial(step_kernel, n), out_shape=shapes, in_sp...  184 us

profile of v4, /device:TPU:33, one launch (start us, length us, event | category | flops | bytes accessed | tf_op | source)
XLA Modules:
  0.0 186.5 jit_solution(7777742621048480836)
XLA Ops:
  0.6 184.2 %mixer_moe_step.1 = (bf16[16,128]{1,0:T(8,128)(2,1)S(1)}, f32[3,256,128]{2,1,0:T(8,128)S(1)}, f32[4,256,128]{2,1,0:T(8,128)S(1)}, f32[1,8]{1,0:T(1,128)S(1)}, f32[1,1]{1,0:T(1,128)}) custom-call(bf16[16,128]{1,0:T(8,128)(2,1)} %bitcast.29, f32[3,256,128]{2,1,0:T(8,128)} %cs_hbm.1, f32[8,2048]{1,0:T(8,128)} %bitcast.27, f32[4,128]{1,0:T(4,128)} %bitcast.30, ...), custom_call_target="tpu_custom_call" | custom-call | tf_op jit(solution)/shard_map/mixer_moe_step/pallas_call | solution.py:628
  184.9 1.6 finish.1

commit v5 on v4

--- a/solution.py
+++ b/solution.py
@@ -81,7 +81,7 @@
     (
         cs, rw, pick, pick_row, G, XC, XG, XS, cob, P2, R2, F2, S2, XR, N3, R3, F3, Q3, ST, F4, G4, rows,
         rn, X5, Y5, N5, R5, F5, Q5, AN, AF, send_sem, recv_sem, piece_sem, up_send, up_recv, down_send,
-        down_recv, wrap_sem, ready_up, ready_wrap, ready_near, load_sem,
+        down_recv, onward_send, wrap_sem, ready_up, ready_wrap, ready_zero, ready_near, load_sem,
     ) = refs[2 * count + 5 :]
     head = lax.axis_index("head")
     x = lax.axis_index("state")
@@ -107,9 +107,12 @@
         greet(side[k])
     for other in around:
         pl.when(other > head)(functools.partial(greet, {"head": other}))
-    for k in range(1, NB):
-        pl.when(b + k < NB)(functools.partial(greet, {"head": (b + k) * NM + m}))
-    expected = b + (X - 1)
+    top = NB - 1
+    for k in range(1, NB - 1):
+        pl.when((b > 0) & (b + k < NB))(functools.partial(greet, {"head": (b + k) * NM + m}))
+    pl.when(b == 0)(functools.partial(greet, {"head": top * NM + m}))
+    pl.when(b == 1)(functools.partial(greet, {"head": m}))
+    expected = (X - 1) + jnp.where(b == 0, 1, b - 1) + jnp.where(b == top, 1, 0)
     for other in around:
         expected += jnp.where(other < head, 1, 0)
 
@@ -179,9 +182,13 @@
     loaded("tok")
     pl.semaphore_wait(barrier, expected)
 
-    @pl.when(b > 0)
+    @pl.when(b > 1)
     def _():
         pl.semaphore_signal(ready_up, inc=1, device_id={"head": head - NM}, device_id_type=MESH)
+
+    @pl.when(b == 0)
+    def _():
+        pl.semaphore_signal(ready_zero, inc=1, device_id={"head": head + NM}, device_id_type=MESH)
 
     for k in near:
         source = (head + n.H - offset(k)) % n.H
@@ -196,7 +203,7 @@
     downs = []
     for k in by_distance(NB):
         copy = remote(own, own, down_send.at[k - 1], down_recv.at[k - 1], {"head": head - k * NM})
-        pl.when(b >= k)(copy.start)
+        pl.when(b > k)(copy.start)
         downs.append((k, copy))
     climbing = b < NB - 1
     ups = [
@@ -204,11 +211,10 @@
         for k in range(NB - 1)
     ]
 
-    @pl.when(climbing)
+    @pl.when((b > 0) & climbing)
     def _():
         pl.semaphore_wait(ready_up, 1)
 
-    top = NB - 1
     around_top = remote(G.at[m, 0], G.at[m, 0], wrap_sem.at[0], wrap_sem.at[1], {"head": top * NM + m})
     descent = remote(G.at[m, 0], G.at[m, 0], wrap_sem.at[0], wrap_sem.at[1], {"head": head - NM})
     below = b < NB // 2
@@ -236,9 +242,21 @@
         around_top.wait_recv()
         pl.when(b > NB // 2 + 1)(descent.start)
 
+    onward = [
+        remote(G.at[m, k], G.at[m, k], onward_send.at[k - 1], down_recv.at[k - 1], {"head": head - NM})
+        for k in range(1, NB)
+    ]
+
     def from_above(last):
         for k, copy in sorted(downs, key=lambda t: t[0]):
             pl.when((b + k == NB - 1) if last else (b + k < NB - 1))(copy.wait_recv)
+            if (k == NB - 2) == last and k < NB - 1:
+                pl.when(b == 1)(onward[k].start)
+
+    @pl.when(b == 1)
+    def _():
+        pl.semaphore_wait(ready_zero, 1)
+        onward[0].start()
 
     def near_ready(k):
         target = (head + n.H + offset(k)) % n.H
@@ -534,7 +552,8 @@
     for copy in pending:
         copy.wait()
     for k, copy in downs:
-        pl.when(b >= k)(copy.wait_send)
+        pl.when(b > k)(copy.wait_send)
+        pl.when(b == 1)(onward[k - 1].wait_send)
     for k in range(1, NB - 1):
         pl.when((k <= b) & climbing)(ups[k].wait_send)
     pl.when(below)(ups[0].wait_send)
@@ -615,8 +634,8 @@
     dma, regular = pltpu.SemaphoreType.DMA, pltpu.SemaphoreType.REGULAR
     climb = dma((n.NB - 1,))
     scratch += [
-        dma((len(STAGES),)), dma((len(STAGES),)), dma((2, n.NM - 1)), climb, climb, climb, climb,
-        dma((2,)), regular, regular, regular((n.NM - 1,)), dma((len(OPERANDS) + 4,)),
+        dma((len(STAGES),)), dma((len(STAGES),)), dma((2, n.NM - 1)), climb, climb, climb, climb, climb,
+        dma((2,)), regular, regular, regular, regular((n.NM - 1,)), dma((len(OPERANDS) + 4,)),
     ]
     shapes = (
         jax.ShapeDtypeStruct((n.R, LANES), BF16),

time: 187 us -> 171 us (0.914)
  Pallas kernels: 186 us -> 170 us
    pallas_call x1, Pallas kernels: 184 us -> 168 us  [per_device(): pl.pallas_call(functools.partial(step_kernel, n), out_shape=shapes, in_sp...]
where the time goes in v5:
time: 171 us
  Pallas kernels  170 us (99%)
    pallas_call x1, Pallas kernels, per_device(): pl.pallas_call(functools.partial(step_kernel, n), out_shape=shapes, in_sp...  168 us

profile of v5, /device:TPU:33, one launch (start us, length us, event | category | flops | bytes accessed | tf_op | source)
XLA Modules:
  0.0 170.5 jit_solution(13190073740921611635)
XLA Ops:
  0.6 168.2 %mixer_moe_step.1 = (bf16[16,128]{1,0:T(8,128)(2,1)S(1)}, f32[3,256,128]{2,1,0:T(8,128)S(1)}, f32[4,256,128]{2,1,0:T(8,128)S(1)}, f32[1,8]{1,0:T(1,128)S(1)}, f32[1,1]{1,0:T(1,128)}) custom-call(bf16[16,128]{1,0:T(8,128)(2,1)} %bitcast.29, f32[3,256,128]{2,1,0:T(8,128)} %cs_hbm.1, f32[8,2048]{1,0:T(8,128)} %bitcast.27, f32[4,128]{1,0:T(4,128)} %bitcast.30, ...), custom_call_target="tpu_custom_call" | custom-call | tf_op jit(solution)/shard_map/mixer_moe_step/pallas_call | solution.py:647
  168.9 1.6 finish.1

commit v6 on v5

--- a/solution.py
+++ b/solution.py
@@ -203,7 +203,7 @@
     downs = []
     for k in by_distance(NB):
         copy = remote(own, own, down_send.at[k - 1], down_recv.at[k - 1], {"head": head - k * NM})
-        pl.when(b > k)(copy.start)
+        pl.when((b > k) | (b == k if k == top else False))(copy.start)
         downs.append((k, copy))
     climbing = b < NB - 1
     ups = [
@@ -215,16 +215,19 @@
     def _():
         pl.semaphore_wait(ready_up, 1)
 
-    around_top = remote(G.at[m, 0], G.at[m, 0], wrap_sem.at[0], wrap_sem.at[1], {"head": top * NM + m})
-    descent = remote(G.at[m, 0], G.at[m, 0], wrap_sem.at[0], wrap_sem.at[1], {"head": head - NM})
+    around_top = remote(G.at[m, 0], G.at[m, 0], wrap_sem.at[1], wrap_sem.at[0], {"head": top * NM + m})
+    descents = [
+        remote(G.at[m, 0], G.at[m, 0], wrap_sem.at[1 + k], wrap_sem.at[0], {"head": head - k * NM})
+        for k in range(1, top - NB // 2)
+    ]
     below = b < NB // 2
 
     @pl.when(b == top)
     def _():
         pl.semaphore_signal(ready_wrap, inc=1, device_id={"head": m}, device_id_type=MESH)
         around_top.wait_recv()
-        if top > NB // 2 + 1:
-            descent.start()
+        for copy in descents:
+            copy.start()
 
     for k in range(NB - 2, 0, -1):
         pl.when(k < b)(ups[k].wait_recv)
@@ -240,17 +243,16 @@
     @pl.when((b > NB // 2) & (b < top))
     def _():
         around_top.wait_recv()
-        pl.when(b > NB // 2 + 1)(descent.start)
 
     onward = [
         remote(G.at[m, k], G.at[m, k], onward_send.at[k - 1], down_recv.at[k - 1], {"head": head - NM})
-        for k in range(1, NB)
+        for k in range(1, top)
     ]
 
     def from_above(last):
         for k, copy in sorted(downs, key=lambda t: t[0]):
             pl.when((b + k == NB - 1) if last else (b + k < NB - 1))(copy.wait_recv)
-            if (k == NB - 2) == last and k < NB - 1:
+            if not last and k < top - 1:
                 pl.when(b == 1)(onward[k].start)
 
     @pl.when(b == 1)
@@ -272,17 +274,17 @@
     )
     tok_bf = G[m, b]
 
-    r_i, c_i = grid_of(T, n.H * R)
-    tok_of = (div(mod(c_i, NB * R), R) * NM + div(c_i, NB * R)) * OWN + mod(c_i, OWN)
-    match = tok_of == r_i
-    which = mod(div(c_i, OWN), J)
-    for j in range(J):
-        pick[j] = ones_where(match & (which == j))
-    r_i, c_i = grid_of(n.SLOTS, n.SLOTS * J)
-    match = div(c_i, J * CAP) * CAP + mod(c_i, CAP) == r_i
-    which = mod(div(c_i, CAP), J)
-    for j in range(J):
-        pick_row[j] = ones_where(match & (which == j))
+    per = NM * OWN
+    r_i, c_i = grid_of(NM * R, NM * R)
+    pick[...] = ones_where(
+        (mod(div(c_i, OWN), J) == div(r_i, per)) & (div(c_i, R) * OWN + mod(c_i, OWN) == mod(r_i, per))
+    )
+    pair = 2 * NB * CAP
+    r_i, c_i = grid_of(pair * J, pair * J)
+    pick_row[...] = ones_where(
+        (mod(div(c_i, CAP), J) == div(r_i, pair))
+        & (div(c_i, J * CAP) * CAP + mod(c_i, CAP) == mod(r_i, pair))
+    )
 
     from_above(True)
     final = G.at[m, NB - 1]
@@ -291,12 +293,12 @@
     arrive(sent_early)
     arrive(sent)
 
-    gathered = G[...].reshape(n.H * R, LANES)
+    by_block = [mm(pick[...], G[:, k].reshape(NM * R, LANES)) for k in range(NB)]
     conv_part = jnp.zeros((T, C), F32)
     gate_part = jnp.zeros((T, C), F32)
     squares = jnp.zeros((T, 1), F32)
     for j in range(J):
-        tok_j = mm(pick[j], gathered)
+        tok_j = jnp.concatenate([rows_k[j * per : (j + 1) * per] for rows_k in by_block], axis=0)
         squares += jnp.sum(tok_j * tok_j, axis=1, keepdims=True)
         wide = tok_j * mixn_ref[j : j + 1, :]
         high = wide.astype(BF16)
@@ -499,9 +501,12 @@
     squares = jnp.zeros((n.SLOTS, 1), F32)
     for k in range(X):
         source = G4[k].astype(F32).reshape(n.SLOTS * J, LANES).astype(BF16)
+        by_pair = [
+            mm(pick_row[...], source[at : at + pair * J]) for at in range(0, n.SLOTS * J, pair * J)
+        ]
         for j in range(J):
             at = k * J + j
-            part = mm(pick_row[j], source)
+            part = jnp.concatenate([rows_k[j * pair : (j + 1) * pair] for rows_k in by_pair], axis=0)
             squares += jnp.sum(part * part, axis=1, keepdims=True)
             rows[:, at * LANES : (at + 1) * LANES] = part * mn_ref[at : at + 1, :]
     inv_rows = lax.rsqrt(squares / n.D + NORM_EPS)
@@ -552,12 +557,15 @@
     for copy in pending:
         copy.wait()
     for k, copy in downs:
-        pl.when(b > k)(copy.wait_send)
-        pl.when(b == 1)(onward[k - 1].wait_send)
+        pl.when((b > k) | (b == k if k == top else False))(copy.wait_send)
+        if k < top:
+            pl.when(b == 1)(onward[k - 1].wait_send)
     for k in range(1, NB - 1):
         pl.when((k <= b) & climbing)(ups[k].wait_send)
     pl.when(below)(ups[0].wait_send)
-    pl.when((b == 0) | (b > NB // 2 + 1))(around_top.wait_send)
+    pl.when(b == 0)(around_top.wait_send)
+    for copy in descents:
+        pl.when(b == top)(copy.wait_send)
 
 
 def finish_kernel(*refs):
@@ -612,8 +620,8 @@
     scratch = [V(a.shape, a.dtype) for a in operands]
     scratch += [
         V(conv_state.shape[1:], F32), V((EXPERTS, n.Q), F32),
-        V((n.J, n.T, n.H * n.R), BF16),
-        V((n.J, n.SLOTS, n.SLOTS * n.J), BF16),
+        V((n.NM * n.R, n.NM * n.R), BF16),
+        V((2 * n.NB * wide, 2 * n.NB * wide), BF16),
         V((n.NM, n.NB, n.R, LANES), BF16),
         V((n.X, n.T, n.C), BF16), V((n.X, n.T, n.C), BF16),
         V((n.X, 8, n.T), F32),
@@ -635,7 +643,7 @@
     climb = dma((n.NB - 1,))
     scratch += [
         dma((len(STAGES),)), dma((len(STAGES),)), dma((2, n.NM - 1)), climb, climb, climb, climb, climb,
-        dma((2,)), regular, regular, regular, regular((n.NM - 1,)), dma((len(OPERANDS) + 4,)),
+        dma((n.NB,)), regular, regular, regular, regular((n.NM - 1,)), dma((len(OPERANDS) + 4,)),
     ]
     shapes = (
         jax.ShapeDtypeStruct((n.R, LANES), BF16),

time: 171 us -> 170 us (level)
  Pallas kernels: 170 us -> 168 us
where the time goes in v6:
time: 170 us; the launch traced here: 169 us
  Pallas kernels  168 us (99%)
    pallas_call x1, Pallas kernels, per_device(): pl.pallas_call(functools.partial(step_kernel, n), out_shape=shapes, in_sp...  167 us

profile of v6, /device:TPU:33, one launch (start us, length us, event | category | flops | bytes accessed | tf_op | source)
XLA Modules:
  0.0 168.9 jit_solution(17500214607203604453)
XLA Ops:
  0.6 166.7 %mixer_moe_step.1 = (bf16[16,128]{1,0:T(8,128)(2,1)S(1)}, f32[3,256,128]{2,1,0:T(8,128)S(1)}, f32[4,256,128]{2,1,0:T(8,128)S(1)}, f32[1,8]{1,0:T(1,128)S(1)}, f32[1,1]{1,0:T(1,128)}) custom-call(bf16[16,128]{1,0:T(8,128)(2,1)} %bitcast.29, f32[3,256,128]{2,1,0:T(8,128)} %cs_hbm.1, f32[8,2048]{1,0:T(8,128)} %bitcast.27, f32[4,128]{1,0:T(4,128)} %bitcast.30, ...), custom_call_target="tpu_custom_call" | custom-call | tf_op jit(solution)/shard_map/mixer_moe_step/pallas_call | solution.py:655
  167.3 1.6 finish.1

commit v7 on v6

--- a/solution.py
+++ b/solution.py
@@ -64,7 +64,7 @@
 
 STAGES = (
     "tok_near", "tok_last", "branch", "gate", "square", "proj_near", "proj_far", "low_near", "low_state",
-    "read", "mix_near", "mix_far", "stat", "row_far", "row_near", "row_state", "out_state", "out_near",
+    "read", "mix_near", "mix_far", "stat", "row_far", "row_near", "row_state", "out_pair", "out_state", "out_near",
     "out_far", "aux_near", "aux_far",
 )
 OPERANDS = (
@@ -80,7 +80,7 @@
     held = dict(zip(OPERANDS, refs[count + 5 : 2 * count + 5]))
     (
         cs, rw, pick, pick_row, G, XC, XG, XS, cob, P2, R2, F2, S2, XR, N3, R3, F3, Q3, ST, F4, G4, rows,
-        rn, X5, Y5, N5, R5, F5, Q5, AN, AF, send_sem, recv_sem, piece_sem, up_send, up_recv, down_send,
+        rn, X5, W5, V5, Y5, N5, R5, F5, Q5, AN, AF, send_sem, recv_sem, piece_sem, up_send, up_recv, down_send,
         down_recv, onward_send, wrap_sem, ready_up, ready_wrap, ready_zero, ready_near, load_sem,
     ) = refs[2 * count + 5 :]
     head = lax.axis_index("head")
@@ -96,6 +96,14 @@
     near = {k: {"head": (head + n.H + offset(k)) % n.H} for k in range(1, NM)}
     block = {k: {"head": b * NM + (m + k) % NM} for k in range(1, NM)}
     side = {k: {"state": (x + k) % X} for k in range(1, X)}
+
+    loads = {}
+
+    def load(name, src, dst):
+        loads[name] = pltpu.make_async_copy(src, dst, load_sem.at[len(loads)])
+        loads[name].start()
+
+    load("tok", tok_hbm, G.at[m, b])
 
     barrier = pltpu.get_barrier_semaphore()
     around = [(head + n.H + o) % n.H for o in range(-(NM // 2), NM // 2 + 1) if o]
@@ -116,13 +124,6 @@
     for other in around:
         expected += jnp.where(other < head, 1, 0)
 
-    loads = {}
-
-    def load(name, src, dst):
-        loads[name] = pltpu.make_async_copy(src, dst, load_sem.at[len(loads)])
-        loads[name].start()
-
-    load("tok", tok_hbm, G.at[m, b])
     for name, src in zip(OPERANDS, sources):
         load(name, src, held[name])
     load("conv", cs_hbm.at[0], cs)
@@ -506,7 +507,10 @@
         ]
         for j in range(J):
             at = k * J + j
-            part = jnp.concatenate([rows_k[j * pair : (j + 1) * pair] for rows_k in by_pair], axis=0)
+            starts = [j * pair + c * NB * CAP for c in range(2)]
+            part = jnp.concatenate(
+                [rows_k[start : start + NB * CAP] for start in starts for rows_k in by_pair], axis=0
+            )
             squares += jnp.sum(part * part, axis=1, keepdims=True)
             rows[:, at * LANES : (at + 1) * LANES] = part * mn_ref[at : at + 1, :]
     inv_rows = lax.rsqrt(squares / n.D + NORM_EPS)
@@ -514,24 +518,41 @@
     normed = rn[...]
     hidden = (silu(mm_nt(normed, held["gp"][0])) * mm_nt(normed, held["up"][0])).astype(BF16)
 
-    def down_part(k):
+    core, half = m % 2, n.SLOTS // 2
+    pair_at = STAGES.index("out_pair")
+    for k in by_distance(X) + [0]:
         at = (x + k) % X
         columns = pl.ds(pl.multiple_of(at * n.Q, n.Q), n.Q)
-        X5[at] = mm(hidden, held["dn"][0, :, columns]).astype(BF16)
-
-    sent = exchange("out_state", side, lambda k: (X5.at[(x + k) % X], Y5.at[x]), Y5.at[0 : X - 1], down_part)
-    down_part(0)
-    Y5[x] = X5[x]
+        X5[at] = mm(hidden, held["dn"][0, :, columns]).astype(BF16).reshape(2, half, n.Q)
+        remote(
+            X5.at[at, 1 - core], W5.at[at], send_sem.at[pair_at], recv_sem.at[pair_at],
+            {"head": head + 1 - 2 * core},
+        ).start()
+    pending.append(pltpu.make_async_copy(W5, W5, send_sem.at[pair_at]))
+    arrive(pltpu.make_async_copy(W5, W5, recv_sem.at[pair_at]))
+
+    def both(k):
+        at = (x + k) % X
+        V5[at] = (X5[at, core].astype(F32) + W5[at].astype(F32)).astype(BF16)
+
+    sent = exchange("out_state", side, lambda k: (V5.at[(x + k) % X], Y5.at[x]), Y5.at[0 : X - 1], both)
+    both(0)
+    Y5[x] = V5[x]
     arrive(sent)
     total = Y5[0].astype(F32)
     for k in range(1, X):
         total += Y5[k].astype(F32)
-    N5[...] = total.reshape(NM, NB * CAP, n.Q).astype(BF16)
-    R5[m] = N5[m]
-    sent = exchange("out_near", block, lambda k: (N5.at[(m + k) % NM], R5.at[m]), R5.at[0 : NM - 1])
-    arrive(sent)
+    chips, chip = NM // 2, m // 2
+    N5[...] = total.astype(BF16).reshape(chips, NB * CAP, n.Q)
+    R5[chip] = N5[chip]
+    if chips > 1:
+        alike = {k: {"head": b * NM + (chip + k) % chips * 2 + core} for k in range(1, chips)}
+        sent = exchange(
+            "out_near", alike, lambda k: (N5.at[(chip + k) % chips], R5.at[chip]), R5.at[0 : chips - 1]
+        )
+        arrive(sent)
     total = R5[0].astype(F32)
-    for k in range(1, NM):
+    for k in range(1, chips):
         total += R5[k].astype(F32)
     total = total.astype(BF16)
     r_i, c_i = grid_of(NB * J * CAP, NB * CAP)
@@ -634,8 +655,9 @@
         V((n.X, n.R, LANES), F32),
         V((n.NB, wide, LANES), BF16), V((n.X, n.NM, n.NB, wide, LANES), BF16),
         V((n.SLOTS, n.D), F32), V((n.SLOTS, n.D), BF16),
-        V((n.X, n.SLOTS, n.Q), BF16), V((n.X, n.SLOTS, n.Q), BF16),
-        V((n.NM, n.NB * CAP, n.Q), BF16), V((n.NM, n.NB * CAP, n.Q), BF16),
+        V((n.X, 2, n.SLOTS // 2, n.Q), BF16), V((n.X, n.SLOTS // 2, n.Q), BF16),
+        V((n.X, n.SLOTS // 2, n.Q), BF16), V((n.X, n.SLOTS // 2, n.Q), BF16),
+        V((n.NM // 2, n.NB * CAP, n.Q), BF16), V((n.NM // 2, n.NB * CAP, n.Q), BF16),
         V((n.NB, wide, LANES), BF16), V((n.NB, wide, LANES), BF16),
         V((n.NM, 8, LANES), F32), V((n.NB, 8, LANES), F32),
     ]

time: 170 us -> 168 us (0.988)
  Pallas kernels: 168 us -> 166 us
    pallas_call x1, Pallas kernels: 167 us -> 164 us  [per_device(): pl.pallas_call(functools.partial(step_kernel, n), out_shape=shapes, in_sp...]
where the time goes in v7:
time: 168 us; the launch traced here: 167 us
  Pallas kernels  166 us (99%)
    pallas_call x1, Pallas kernels, per_device(): pl.pallas_call(functools.partial(step_kernel, n), out_shape=shapes, in_sp...  164 us

profile of v7, /device:TPU:33, one launch (start us, length us, event | category | flops | bytes accessed | tf_op | source)
XLA Modules:
  0.0 166.7 jit_solution(247562176150390708)
XLA Ops:
  0.6 164.4 %mixer_moe_step.1 = (bf16[16,128]{1,0:T(8,128)(2,1)S(1)}, f32[3,256,128]{2,1,0:T(8,128)S(1)}, f32[4,256,128]{2,1,0:T(8,128)S(1)}, f32[1,8]{1,0:T(1,128)S(1)}, f32[1,1]{1,0:T(1,128)}) custom-call(bf16[16,128]{1,0:T(8,128)(2,1)} %bitcast.29, f32[3,256,128]{2,1,0:T(8,128)} %cs_hbm.1, f32[8,2048]{1,0:T(8,128)} %bitcast.27, f32[4,128]{1,0:T(4,128)} %bitcast.30, ...), custom_call_target="tpu_custom_call" | custom-call | tf_op jit(solution)/shard_map/mixer_moe_step/pallas_call | solution.py:677
  165.1 1.6 finish.1

commit v8 on v7

--- a/solution.py
+++ b/solution.py
@@ -64,7 +64,7 @@
 
 STAGES = (
     "tok_near", "tok_last", "branch", "gate", "square", "proj_near", "proj_far", "low_near", "low_state",
-    "read", "mix_near", "mix_far", "stat", "row_far", "row_near", "row_state", "out_pair", "out_state", "out_near",
+    "read", "mix_near", "mix_far", "stat", "row_far", "row_near", "row_state", "row_pair", "out_pair", "out_state", "out_near",
     "out_far", "aux_near", "aux_far",
 )
 OPERANDS = (
@@ -157,28 +157,29 @@
     def arrive(copy):
         copy.wait()
 
-    def by_pieces(name, group, ref, at):
+    def by_pieces(name, group, view, own, count, near_landing, side_landing, at):
         near_at, side_at = STAGES.index(name + "_near"), STAGES.index(name + "_state")
         sent = {}
-        order = by_distance(NM)
+        order = by_distance(count)
         for k in order:
-            sent[k] = remote(
-                ref.at[x, m], ref.at[x, m], send_sem.at[near_at], piece_sem.at[at, k - 1], group[k]
-            )
+            sent[k] = remote(view(own), view(own), send_sem.at[near_at], piece_sem.at[at, k - 1], group[k])
             sent[k].start()
         for step in [0] + order[::-1]:
-            piece = (m + NM - step) % NM
+            piece = (own + count - step) % count
             if step:
                 sent[step].wait_recv()
             for k in by_distance(X):
                 remote(
-                    ref.at[x, piece], ref.at[x, piece], send_sem.at[side_at], recv_sem.at[side_at], side[k]
+                    view(piece), view(piece), send_sem.at[side_at], recv_sem.at[side_at], side[k]
                 ).start()
-        landing = ref.at[0, 0 : NM - 1]
-        pending.append(pltpu.make_async_copy(landing, landing, send_sem.at[near_at]))
-        landing = ref.at[0 : X - 1]
-        pending.append(pltpu.make_async_copy(landing, landing, send_sem.at[side_at]))
-        return pltpu.make_async_copy(landing, landing, recv_sem.at[side_at])
+        if order:
+            pending.append(pltpu.make_async_copy(near_landing, near_landing, send_sem.at[near_at]))
+        pending.append(pltpu.make_async_copy(side_landing, side_landing, send_sem.at[side_at]))
+        return pltpu.make_async_copy(side_landing, side_landing, recv_sem.at[side_at])
+
+    core, chip, chips = m % 2, m // 2, NM // 2
+    partner = {"head": head + 1 - 2 * core}
+    alike = {k: {"head": b * NM + (chip + k) % chips * 2 + core} for k in range(1, chips)}
 
     loaded("tok")
     pl.semaphore_wait(barrier, expected)
@@ -362,7 +363,7 @@
     _, l_i = grid_of(n.TB, LANES)
     vectors = jnp.where(l_i < spare, vectors, 0.0)
     S2[x, m] = in_halves(jnp.concatenate([low * step_inv * sg_ref[...], vectors], axis=1))
-    sent = by_pieces("low", near, S2, 0)
+    sent = by_pieces("low", near, lambda p: S2.at[x, p], m, NM, S2.at[0, 0 : NM - 1], S2.at[0 : X - 1], 0)
     arrive(sent_gate)
     gate = gate_part
     for k in range(1, X):
@@ -400,28 +401,22 @@
     N3[...] = mm(act, op[...]).astype(BF16).reshape(NM, NB * OWN, n.Q)
     R3[m] = N3[m]
     sent = exchange("mix_near", near, lambda k: (N3.at[(m + k) % NM], R3.at[m]), R3.at[0 : NM - 1])
+    r_i, c_i = grid_of(NB * R, NB * OWN)
+    match = div(r_i, R) * OWN + mod(r_i, OWN) == c_i
+    which = mod(div(r_i, OWN), J)
+    to_owner = [ones_where(match & (which == j)) for j in range(J)]
     arrive(sent)
     total = R3[0].astype(F32)
     for k in range(1, NM):
         total += R3[k].astype(F32)
     total = total.astype(BF16)
-    r_i, c_i = grid_of(NB * R, NB * OWN)
-    match = div(r_i, R) * OWN + mod(r_i, OWN) == c_i
-    which = mod(div(r_i, OWN), J)
     spread = jnp.zeros((NB * R, LANES), F32)
     for j in range(J):
-        spread += mm(ones_where(match & (which == j)), total[:, j * LANES : (j + 1) * LANES])
+        spread += mm(to_owner[j], total[:, j * LANES : (j + 1) * LANES])
     F3[...] = spread.astype(BF16).reshape(NB, R, LANES)
     Q3[b] = F3[b]
     sent = exchange("mix_far", far, lambda k: (F3.at[(b + k) % NB], Q3.at[b]), Q3.at[0 : NB - 1])
     loaded("router", "mn", "eid", "sid")
-    arrive(sent)
-    total = Q3[0].astype(F32)
-    for k in range(1, NB):
-        total += Q3[k].astype(F32)
-
-    resid_bf = (tok_bf.astype(F32) + total).astype(BF16)
-    resid = resid_bf.astype(F32)
     row_i, lane_i = grid_of(R, LANES)
     hits, kept, slots = [], [], []
     i_i, t_i = grid_of(R, OWN)
@@ -443,10 +438,18 @@
     chosen_rows = jnp.where(
         mod(div(d_i, CAP), J) == div(c_i, OWN), mm_nt(slot_of, dispatch), 0.0
     ).astype(BF16)
+    arrive(sent)
+    total = Q3[0].astype(F32)
+    for k in range(1, NB):
+        total += Q3[k].astype(F32)
+
+    resid_bf = (tok_bf.astype(F32) + total).astype(BF16)
+    resid = resid_bf.astype(F32)
     F4[...] = mm(chosen_rows, resid_bf).reshape(NB, J * CAP, LANES).astype(BF16)
-    G4[x, m, b] = F4[b]
+    G4[x, core, chip, b] = F4[b]
+    own = G4.at[x, core, chip, b]
     sent = exchange(
-        "row_far", far, lambda k: (F4.at[(b + k) % NB], G4.at[x, m, b]), G4.at[x, m, 0 : NB - 1]
+        "row_far", far, lambda k: (F4.at[(b + k) % NB], own), G4.at[x, core, chip, 0 : NB - 1]
     )
 
     gain = jnp.zeros((R, LANES), F32)
@@ -490,7 +493,17 @@
 
     arrive(sent)
 
-    sideways = by_pieces("row", block, G4, 1)
+    sideways = by_pieces(
+        "row", alike, lambda p: G4.at[x, core, p], chip, chips, G4.at[0, 0, 0 : chips - 1],
+        G4.at[0 : X - 1, 0], 1,
+    )
+    pair_at = STAGES.index("row_pair")
+
+    def swap(at):
+        rows_at = G4.at[at, core]
+        remote(rows_at, rows_at, send_sem.at[pair_at], recv_sem.at[pair_at], partner).start()
+
+    swap(x)
     arrive(sent_aux)
     total = AN[0]
     for k in range(1, NM):
@@ -498,6 +511,11 @@
     AF[b] = total
     sent_aux = exchange("aux_far", far, lambda k: (AF.at[b], AF.at[b]), AF.at[0 : NB - 1])
     arrive(sideways)
+    for k in range(1, X):
+        swap((x + k) % X)
+    landing = G4.at[0:X, 0]
+    pending.append(pltpu.make_async_copy(landing, landing, send_sem.at[pair_at]))
+    arrive(pltpu.make_async_copy(landing, landing, recv_sem.at[pair_at]))
 
     squares = jnp.zeros((n.SLOTS, 1), F32)
     for k in range(X):
@@ -507,10 +525,7 @@
         ]
         for j in range(J):
             at = k * J + j
-            starts = [j * pair + c * NB * CAP for c in range(2)]
-            part = jnp.concatenate(
-                [rows_k[start : start + NB * CAP] for start in starts for rows_k in by_pair], axis=0
-            )
+            part = jnp.concatenate([rows_k[j * pair : (j + 1) * pair] for rows_k in by_pair], axis=0)
             squares += jnp.sum(part * part, axis=1, keepdims=True)
             rows[:, at * LANES : (at + 1) * LANES] = part * mn_ref[at : at + 1, :]
     inv_rows = lax.rsqrt(squares / n.D + NORM_EPS)
@@ -518,7 +533,7 @@
     normed = rn[...]
     hidden = (silu(mm_nt(normed, held["gp"][0])) * mm_nt(normed, held["up"][0])).astype(BF16)
 
-    core, half = m % 2, n.SLOTS // 2
+    half = n.SLOTS // 2
     pair_at = STAGES.index("out_pair")
     for k in by_distance(X) + [0]:
         at = (x + k) % X
@@ -526,7 +541,7 @@
         X5[at] = mm(hidden, held["dn"][0, :, columns]).astype(BF16).reshape(2, half, n.Q)
         remote(
             X5.at[at, 1 - core], W5.at[at], send_sem.at[pair_at], recv_sem.at[pair_at],
-            {"head": head + 1 - 2 * core},
+            partner,
         ).start()
     pending.append(pltpu.make_async_copy(W5, W5, send_sem.at[pair_at]))
     arrive(pltpu.make_async_copy(W5, W5, recv_sem.at[pair_at]))
@@ -538,15 +553,17 @@
     sent = exchange("out_state", side, lambda k: (V5.at[(x + k) % X], Y5.at[x]), Y5.at[0 : X - 1], both)
     both(0)
     Y5[x] = V5[x]
+    r_i, c_i = grid_of(NB * J * CAP, NB * CAP)
+    match = div(r_i, J * CAP) * CAP + mod(r_i, CAP) == c_i
+    which = mod(div(r_i, CAP), J)
+    to_home = [ones_where(match & (which == j)) for j in range(J)]
     arrive(sent)
     total = Y5[0].astype(F32)
     for k in range(1, X):
         total += Y5[k].astype(F32)
-    chips, chip = NM // 2, m // 2
     N5[...] = total.astype(BF16).reshape(chips, NB * CAP, n.Q)
     R5[chip] = N5[chip]
     if chips > 1:
-        alike = {k: {"head": b * NM + (chip + k) % chips * 2 + core} for k in range(1, chips)}
         sent = exchange(
             "out_near", alike, lambda k: (N5.at[(chip + k) % chips], R5.at[chip]), R5.at[0 : chips - 1]
         )
@@ -555,12 +572,9 @@
     for k in range(1, chips):
         total += R5[k].astype(F32)
     total = total.astype(BF16)
-    r_i, c_i = grid_of(NB * J * CAP, NB * CAP)
-    match = div(r_i, J * CAP) * CAP + mod(r_i, CAP) == c_i
-    which = mod(div(r_i, CAP), J)
     spread = jnp.zeros((NB * J * CAP, LANES), F32)
     for j in range(J):
-        spread += mm(ones_where(match & (which == j)), total[:, j * LANES : (j + 1) * LANES])
+        spread += mm(to_home[j], total[:, j * LANES : (j + 1) * LANES])
     F5[...] = spread.reshape(NB, J * CAP, LANES).astype(BF16)
     Q5[b] = F5[b]
     sent = exchange("out_far", far, lambda k: (F5.at[(b + k) % NB], Q5.at[b]), Q5.at[0 : NB - 1])
@@ -653,7 +667,7 @@
         V((n.NM, n.NB * n.OWN, n.Q), BF16), V((n.NM, n.NB * n.OWN, n.Q), BF16),
         V((n.NB, n.R, LANES), BF16), V((n.NB, n.R, LANES), BF16),
         V((n.X, n.R, LANES), F32),
-        V((n.NB, wide, LANES), BF16), V((n.X, n.NM, n.NB, wide, LANES), BF16),
+        V((n.NB, wide, LANES), BF16), V((n.X, 2, n.NM // 2, n.NB, wide, LANES), BF16),
         V((n.SLOTS, n.D), F32), V((n.SLOTS, n.D), BF16),
         V((n.X, 2, n.SLOTS // 2, n.Q), BF16), V((n.X, n.SLOTS // 2, n.Q), BF16),
         V((n.X, n.SLOTS // 2, n.Q), BF16), V((n.X, n.SLOTS // 2, n.Q), BF16),

time: 168 us -> 165 us (0.982)
  Pallas kernels: 166 us -> 162 us
    pallas_call x1, Pallas kernels: 164 us -> 161 us  [per_device(): pl.pallas_call(functools.partial(step_kernel, n), out_shape=shapes, in_sp...]
where the time goes in v8:
time: 165 us; the launch traced here: 163 us
  Pallas kernels  162 us (98%)
    pallas_call x1, Pallas kernels, per_device(): pl.pallas_call(functools.partial(step_kernel, n), out_shape=shapes, in_sp...  161 us

profile of v8, /device:TPU:33, one launch (start us, length us, event | category | flops | bytes accessed | tf_op | source)
XLA Modules:
  0.0 162.9 jit_solution(2797493027277199697)
XLA Ops:
  0.6 160.6 %mixer_moe_step.1 = (bf16[16,128]{1,0:T(8,128)(2,1)S(1)}, f32[3,256,128]{2,1,0:T(8,128)S(1)}, f32[4,256,128]{2,1,0:T(8,128)S(1)}, f32[1,8]{1,0:T(1,128)S(1)}, f32[1,1]{1,0:T(1,128)}) custom-call(bf16[16,128]{1,0:T(8,128)(2,1)} %bitcast.29, f32[3,256,128]{2,1,0:T(8,128)} %cs_hbm.1, f32[8,2048]{1,0:T(8,128)} %bitcast.27, f32[4,128]{1,0:T(4,128)} %bitcast.30, ...), custom_call_target="tpu_custom_call" | custom-call | tf_op jit(solution)/shard_map/mixer_moe_step/pallas_call | solution.py:691
  161.2 1.6 finish.1
